TPU v7x, 32 devices: a whole 2x2x4 slice. The times are simulated.
32 devices in a mesh: dp: 8 (over z, x), expert: 4 (over y, core).
Axes of the slice: x: 2, y: 2, z: 4, core: 2. Of those that a mesh axis runs over, the one named last changes fastest.
Arguments:
- local_grads: bfloat16 [8, 4, 4, 524288], P('dp', 'expert')
- master_weights: float32 [4, 4, 524288], P('expert', None, 'dp'), may hold values from -6 to 6
- first_moment: float32 [4, 4, 524288], P('expert', None, 'dp')
- second_moment: float32 [4, 4, 524288], P('expert', None, 'dp')
Outputs:
- new_params: bfloat16 [4, 4, 524288], P('expert')
- new_master: float32 [4, 4, 524288], P('expert', None, 'dp')
- new_first: float32 [4, 4, 524288], P('expert', None, 'dp')
- new_second: float32 [4, 4, 524288], P('expert', None, 'dp')
All inputs are finite; a program needn't handle non-finite values.
Results may differ from a plain program's by a relative error of at most 0.0013.
Values may be sent and summed in bfloat16 or wider, within the bound.
A program may use at most 128 MiB of HBM per device.

v0:
```python
import functools

import jax
import jax.numpy as jnp
from jax import lax
from jax.experimental import pallas as pl
from jax.experimental.pallas import tpu as pltpu
from jax.sharding import PartitionSpec as P

beta_first = 0.9
beta_second = 0.95
correct_first = 1.0 - 0.9**10
correct_second = 1.0 - 0.95**10
learn_rate = 0.05
decay_rate = 0.1
clip_limit = 1.0
tiny_eps = 1e-08
norm_eps = 1e-06

MESH = pl.DeviceIdType.MESH
F32 = jnp.float32
CHUNKS = 8
HALF = CHUNKS // 2
PIECES = 8
SPARE_BYTES = 4 * 1024 * 1024
BLOCK = 2048


def adam_update(gradient, master, first, second, clip_factor):
    scaled = clip_factor * gradient
    new_first = beta_first * first + (1.0 - beta_first) * scaled
    new_second = beta_second * second + (1.0 - beta_second) * scaled * scaled
    direction = new_first / correct_first / (jnp.sqrt(new_second / correct_second) + tiny_eps)
    new_master = master - learn_rate * (decay_rate * master + direction)
    return (new_master, new_first, new_second)


def kernel(
    Z, X, E, share,
    grads, master_in, first_in, second_in,
    gathered, master, first, second,
    own, xr, low, high, sbuf, norms, norms2,
    own_sem, state_sem, x_send, x_recv, z_send, low_recv, high_recv,
    n_send, n_recv, m_send, m_recv, g_send, g_recv, h_send,
):
    n = Z * X
    dp = lax.axis_index("dp")
    ex = lax.axis_index("expert")
    z, x = dp // X, dp % X
    chunk = share // CHUNKS

    def at_dp(zz, xx):
        return (zz * X + xx, ex)

    def lanes(base, size):
        return pl.ds(pl.multiple_of(base, 128), size)

    barrier = pltpu.get_barrier_semaphore()
    for k in range(1, n):
        pl.semaphore_signal(barrier, inc=1, device_id=((dp + k) % n, ex), device_id_type=MESH)
    for k in range(1, E):
        pl.semaphore_signal(barrier, inc=1, device_id=(dp, (ex + k) % E), device_id_type=MESH)
    pl.semaphore_wait(barrier, n - 1 + E - 1)

    def own_copy(zz):
        return pltpu.make_async_copy(
            grads.at[:, lanes((zz * X + x) * share, share)], own.at[zz], own_sem.at[zz]
        )

    def x_copy(zz, k, c):
        to = (x + k) % X
        return pltpu.make_async_remote_copy(
            src_ref=grads.at[:, lanes((zz * X + to) * share + c * chunk, chunk)],
            dst_ref=xr.at[zz, k - 1, :, lanes(c * chunk, chunk)],
            send_sem=x_send.at[zz, k - 1, c],
            recv_sem=x_recv.at[zz, k - 1, c],
            device_id=at_dp(z, to),
            device_id_type=MESH,
        )

    def for_dest(k, act):
        @pl.when(z + k < Z)
        def _():
            act(z + k)

        if k:
            @pl.when(z - k >= 0)
            def _():
                act(z - k)

    def start_first(zz):
        own_copy(zz).start()

        def body(c, carry):
            for k in range(1, X):
                x_copy(zz, k, c).start()
            return carry

        lax.fori_loop(0, CHUNKS, body, 0)

    for k in range(Z - 1, -1, -1):
        for_dest(k, start_first)
    states = [
        pltpu.make_async_copy(a, b, state_sem.at[i])
        for i, (a, b) in enumerate(((master_in, master), (first_in, first), (second_in, second)))
    ]
    for s in states:
        s.start()

    def z_copy(zz, c, up):
        where = lanes(c * chunk, chunk)
        return pltpu.make_async_remote_copy(
            src_ref=sbuf.at[zz, :, where],
            dst_ref=(low if up else high).at[zz, :, where],
            send_sem=z_send.at[zz, c],
            recv_sem=(low_recv if up else high_recv).at[zz, c],
            device_id=at_dp(z + 1 if up else z - 1, x),
            device_id_type=MESH,
        )

    def sum_block(zz, where, extras):
        total = own[zz, :, where].astype(F32)
        for k in range(1, X):
            total = total + xr[zz, k - 1, :, where].astype(F32)
        for r in extras:
            total = total + r[zz, :, where]
        return total

    def add_chunk(zz, c, extras):
        def body(b, carry):
            where = lanes(c * chunk + b * BLOCK, BLOCK)
            sbuf[zz, :, where] = sum_block(zz, where, extras)
            return carry

        lax.fori_loop(0, chunk // BLOCK, body, 0)

    def hop(zz, c, up):
        for k in range(1, X):
            x_copy(zz, k, c).wait_recv()
        edge = z == (0 if up else Z - 1)

        @pl.when(edge)
        def _():
            add_chunk(zz, c, ())

        @pl.when(jnp.logical_not(edge))
        def _():
            z_copy(zz, c, up).wait_recv()
            add_chunk(zz, c, (low if up else high,))

        z_copy(zz, c, up).start()

    for k in range(Z - 1, 0, -1):
        for_dest(k, lambda zz: own_copy(zz).wait())

        def body(c, carry, k=k):
            @pl.when(z + k < Z)
            def _():
                hop(z + k, c, True)

            @pl.when(z - k >= 0)
            def _():
                hop(z - k, c, False)

            return carry

        lax.fori_loop(0, CHUNKS, body, 0)

    own_copy(z).wait()
    norms2[0] = jnp.zeros((8, 128), F32)

    def finish_chunk(c, extras):
        def body(b, carry):
            where = lanes(c * chunk + b * BLOCK, BLOCK)
            mean = sum_block(z, where, extras) / n
            sbuf[z, :, where] = mean
            return carry + mean * mean

        squares = lax.fori_loop(0, chunk // BLOCK, body, jnp.zeros((own.shape[1], BLOCK), F32))
        norms2[0] = norms2[0] + jnp.full((8, 128), jnp.sum(squares), F32)

    def finish(c, carry):
        for k in range(1, X):
            x_copy(z, k, c).wait_recv()

        @pl.when(z > 0)
        def _():
            z_copy(z, c, True).wait_recv()

        @pl.when(z < Z - 1)
        def _():
            z_copy(z, c, False).wait_recv()

        @pl.when(z == 0)
        def _():
            finish_chunk(c, (high,))

        @pl.when(z == Z - 1)
        def _():
            finish_chunk(c, (low,))

        @pl.when(jnp.logical_and(z > 0, z < Z - 1))
        def _():
            finish_chunk(c, (low, high))

        return carry

    lax.fori_loop(0, CHUNKS, finish, 0)

    norms[0] = norms2[0]

    def n_copy(k):
        return pltpu.make_async_remote_copy(
            src_ref=norms.at[0], dst_ref=norms.at[k],
            send_sem=n_send.at[k], recv_sem=n_recv.at[k],
            device_id=((dp + k) % n, ex), device_id_type=MESH,
        )

    def m_copy(k):
        return pltpu.make_async_remote_copy(
            src_ref=norms2.at[0], dst_ref=norms2.at[k],
            send_sem=m_send.at[k], recv_sem=m_recv.at[k],
            device_id=(dp, (ex + k) % E), device_id_type=MESH,
        )

    for k in range(1, n):
        n_copy(k).start()
    for s in states:
        s.wait()
    total = norms[0]
    for k in range(1, n):
        n_copy(k).wait_recv()
        total = total + norms[k]
    norms2[0] = total
    for k in range(1, E):
        m_copy(k).start()
    for k in range(1, E):
        m_copy(k).wait_recv()
        total = total + norms2[k]
    clip_all = jnp.minimum(1.0, clip_limit / (jnp.sqrt(total) + norm_eps))
    clip_factor = jnp.max(clip_all)

    def g_copy(zz, c, way):
        where = lanes((zz * X + x) * share + c * chunk, chunk)
        if way < 2:
            target = at_dp(z + 1 if way == 0 else z - 1, x)
        else:
            target = at_dp(z, (x + way - 1) % X)
        return pltpu.make_async_remote_copy(
            src_ref=gathered.at[:, where], dst_ref=gathered.at[:, where],
            send_sem=g_send.at[way, zz, c], recv_sem=g_recv.at[zz * X + x, c],
            device_id=target, device_id_type=MESH,
        )

    def arrived(zz, xx, c):
        where = lanes((zz * X + xx) * share + c * chunk, chunk)
        pltpu.make_async_remote_copy(
            src_ref=gathered.at[:, where], dst_ref=gathered.at[:, where],
            send_sem=g_send.at[0, 0, c], recv_sem=g_recv.at[zz * X + xx, c],
            device_id=(dp, (ex + 1) % E), device_id_type=MESH,
        ).wait_recv()

    pair = z + 1 - 2 * (z % 2)

    def h_copy(k, c):
        where = lanes((z * X + (x + k) % X) * share + c * chunk, chunk)
        return pltpu.make_async_remote_copy(
            src_ref=gathered.at[:, where], dst_ref=gathered.at[:, where],
            send_sem=h_send.at[k - 1, c], recv_sem=g_recv.at[z * X + (x + k) % X, c],
            device_id=at_dp(pair, x), device_id_type=MESH,
        )

    def along_x(zz, c, act):
        @pl.when(jnp.logical_or(zz != pair, c < HALF))
        def _():
            for k in range(1, X):
                act(g_copy(zz, c, k + 1))

    def update(c, carry):
        def body(b, inner):
            where = lanes(c * chunk + b * BLOCK, BLOCK)
            m, f, s = adam_update(
                sbuf[z, :, where], master[:, where], first[:, where], second[:, where], clip_factor
            )
            master[:, where] = m
            first[:, where] = f
            second[:, where] = s
            gathered[:, lanes(dp * share + c * chunk + b * BLOCK, BLOCK)] = m.astype(jnp.bfloat16)
            return inner

        lax.fori_loop(0, chunk // BLOCK, body, 0)

        @pl.when(z < Z - 1)
        def _():
            g_copy(z, c, 0).start()

        @pl.when(z > 0)
        def _():
            g_copy(z, c, 1).start()

        for k in range(1, X):
            g_copy(z, c, k + 1).start()
        return carry

    lax.fori_loop(0, CHUNKS, update, 0)

    for s in range(1, Z):
        def relay(c, carry, s=s):
            @pl.when(z - s >= 0)
            def _():
                arrived(z - s, x, c)

                @pl.when(z < Z - 1)
                def _():
                    g_copy(z - s, c, 0).start()

                along_x(z - s, c, lambda copy: copy.start())

            @pl.when(z + s < Z)
            def _():
                arrived(z + s, x, c)

                @pl.when(z > 0)
                def _():
                    g_copy(z + s, c, 1).start()

                along_x(z + s, c, lambda copy: copy.start())

            return carry

        lax.fori_loop(0, CHUNKS, relay, 0)

        if s == 1:
            def across(c, carry):
                for k in range(1, X):
                    arrived(z, (x + k) % X, c)
                    h_copy(k, c).start()
                return carry

            lax.fori_loop(HALF, CHUNKS, across, 0)

    for s in range(Z):
        def collect(zz, s=s):
            def body(c, carry):
                for k in range(1, X):
                    arrived(zz, (x + k) % X, c)
                return carry

            lax.fori_loop(0, HALF if s == 0 else CHUNKS, body, 0)

        for_dest(s, collect)

    def drain(c, carry):
        for zz in range(Z):
            for k in range(1, X):
                x_copy(zz, k, c).wait_send()
            along_x(zz, c, lambda copy: copy.wait_send())

            @pl.when(zz > z)
            def _():
                z_copy(zz, c, True).wait_send()

            @pl.when(zz < z)
            def _():
                z_copy(zz, c, False).wait_send()

            @pl.when(jnp.logical_and(zz <= z, z < Z - 1))
            def _():
                g_copy(zz, c, 0).wait_send()

            @pl.when(jnp.logical_and(zz >= z, z > 0))
            def _():
                g_copy(zz, c, 1).wait_send()

        @pl.when(c >= HALF)
        def _():
            for k in range(1, X):
                h_copy(k, c).wait_send()

        return carry

    lax.fori_loop(0, CHUNKS, drain, 0)
    for k in range(1, n):
        n_copy(k).wait_send()
    for k in range(1, E):
        m_copy(k).wait_send()


def write_out(count, *refs):
    sources, targets, sem = refs[:count], refs[count : 2 * count], refs[2 * count]

    def copies(i):
        size = sources[i].shape[1] // PIECES
        for p in range(PIECES):
            where = pl.ds(p * size, size)
            yield pltpu.make_async_copy(sources[i].at[:, where], targets[i].at[:, where], sem.at[i, p])

    for i in range(count):
        for copy in copies(i):
            copy.start()
    for i in range(count):
        for copy in copies(i):
            copy.wait()


def split(count):
    rows = 1
    while rows * rows < count:
        rows *= 2
    return rows, count // rows


def shards(Z, X, E, local_grads, master_weights, first_moment, second_moment):
    layers, flat = local_grads.shape[2:]
    n = Z * X
    share = flat // n
    whole = pl.BlockSpec(memory_space=pltpu.HBM)
    piece = jax.ShapeDtypeStruct((layers, share), F32)
    dma = pltpu.SemaphoreType.DMA
    local = pl.BlockSpec(memory_space=pltpu.VMEM)
    shapes = (jax.ShapeDtypeStruct((layers, flat), jnp.bfloat16), piece, piece, piece)
    arrays = (local_grads[0, 0], master_weights[0], first_moment[0], second_moment[0])
    out_bytes = layers * (2 * flat + 3 * 4 * share)
    used_bytes = layers * Z * share * (2 * X + 3 * 4) + out_bytes
    results = pl.pallas_call(
        functools.partial(kernel, Z, X, E, share),
        out_shape=shapes,
        in_specs=[whole] * 4,
        out_specs=(local,) * 4,
        scratch_shapes=[
            pltpu.VMEM((Z, layers, share), jnp.bfloat16),
            pltpu.VMEM((Z, X - 1, layers, share), jnp.bfloat16),
            pltpu.VMEM((Z, layers, share), F32),
            pltpu.VMEM((Z, layers, share), F32),
            pltpu.VMEM((Z, layers, share), F32),
            pltpu.VMEM((n, 8, 128), F32),
            pltpu.VMEM((E, 8, 128), F32),
            dma((Z,)), dma((3,)),
            dma((Z, X - 1, CHUNKS)), dma((Z, X - 1, CHUNKS)),
            dma((Z, CHUNKS)), dma((Z, CHUNKS)), dma((Z, CHUNKS)),
            dma((n,)), dma((n,)), dma((E,)), dma((E,)),
            dma((X + 1, Z, CHUNKS)), dma((n, CHUNKS)), dma((X - 1, CHUNKS)),
        ],
        compiler_params=pltpu.CompilerParams(
            collective_id=0, has_side_effects=True, vmem_limit_bytes=used_bytes + SPARE_BYTES
        ),
    )(*(pltpu.with_memory_space_constraint(a, pltpu.HBM) for a in arrays))
    results = pl.pallas_call(
        functools.partial(write_out, len(shapes)),
        out_shape=shapes,
        in_specs=[local] * 4,
        out_specs=(whole,) * 4,
        scratch_shapes=[dma((len(shapes), PIECES))],
        compiler_params=pltpu.CompilerParams(vmem_limit_bytes=out_bytes + SPARE_BYTES),
    )(*results)
    return tuple(r[None] for r in results)


def solution(mesh):
    Z, X = split(mesh.shape["dp"])
    moments = P("expert", None, "dp")
    return jax.shard_map(
        functools.partial(shards, Z, X, mesh.shape["expert"]),
        mesh=mesh,
        in_specs=(P("dp", "expert", None, None), moments, moments, moments),
        out_specs=(P("expert", None, None), moments, moments, moments),
        check_vma=False,
    )
```

profile of v0, /device:TPU:0, one launch (start us, length us, event | category | flops | bytes accessed | tf_op | source)
XLA Modules:
  0.0 136.0 jit_solution(15331523162908453137)
XLA Ops:
  0.6 132.2 %shard_map.75 = (bf16[4,524288]{1,0:T(4,128)(2,1)S(1)}, f32[4,65536]{1,0:T(4,128)S(1)}, f32[4,65536]{1,0:T(4,128)S(1)}, f32[4,65536]{1,0:T(4,128)S(1)}) custom-call(bf16[4,524288]{1,0:T(4,128)(2,1)} %bitcast.8, f32[4,65536]{1,0:T(4,128)} %bitcast.9, f32[4,65536]{1,0:T(4,128)} %bitcast.10, f32[4,65536]{1,0:T(4,128)} %bitcast.11), custom_call_target="tpu_custom_call" | custom-call | tf_op jit(solution)/shard_map/pallas_call | solution.py:425
  132.8 3.2 %shard_map.76 = (bf16[4,524288]{1,0:T(4,128)(2,1)}, f32[4,65536]{1,0:T(4,128)}, f32[4,65536]{1,0:T(4,128)}, f32[4,65536]{1,0:T(4,128)}) custom-call(bf16[4,524288]{1,0:T(4,128)(2,1)S(1)} %get-tuple-element.12.refs_0_, f32[4,65536]{1,0:T(4,128)S(1)} %get-tuple-element.13.refs_1_, f32[4,65536]{1,0:T(4,128)S(1)} %get-tuple-element.14.refs_2_, ...), custom_call_target="tpu_custom_call" | custom-call | tf_op jit(solution)/shard_map/pallas_call | solution.py:448
where the time goes:
time: 136 us
  Pallas kernels  135 us (99%)
    pallas_call x1, Pallas kernels, shards(): pl.pallas_call(functools.partial(kernel, Z, X, E, share), out_shape=shape...  132 us
    pallas_call x1, Pallas kernels, shards(): pl.pallas_call(functools.partial(write_out, len(shapes)), out_shape=shape...  3.22 us

commit v1 on v0

--- a/solution.py
+++ b/solution.py
@@ -24,6 +24,8 @@
 PIECES = 8
 SPARE_BYTES = 4 * 1024 * 1024
 BLOCK = 2048
+SPAN = 250.0
+TINY = 1e-35
 
 
 def adam_update(gradient, master, first, second, clip_factor):
@@ -35,11 +37,34 @@
     return (new_master, new_first, new_second)
 
 
+def spread_lanes(tile):
+    return jnp.concatenate([tile] * (BLOCK // 128), axis=1)
+
+
+def lane_peak(values):
+    peak = jnp.abs(values)
+    while peak.shape[1] > 128:
+        half = peak.shape[1] // 2
+        peak = jnp.maximum(peak[:, :half], peak[:, half:])
+    return peak
+
+
+def encode(values, scale):
+    size = jnp.exp2(jnp.abs(values) * scale - SPAN / 2)
+    return jnp.where(values < 0, -size, size).astype(jnp.bfloat16)
+
+
+def decode(codes, peak):
+    codes = codes.astype(F32)
+    size = (jnp.log2(jnp.abs(codes)) + SPAN / 2) * spread_lanes(peak.astype(F32) / SPAN)
+    return jnp.where(codes < 0, -size, size)
+
+
 def kernel(
     Z, X, E, share,
     grads, master_in, first_in, second_in,
     gathered, master, first, second,
-    own, xr, low, high, sbuf, norms, norms2,
+    own, xr, low, high, code, exact, mean_grad, norms, norms2,
     own_sem, state_sem, x_send, x_recv, z_send, low_recv, high_recv,
     n_send, n_recv, m_send, m_recv, g_send, g_recv, h_send,
 ):
@@ -108,31 +133,41 @@
         s.start()
 
     def z_copy(zz, c, up):
-        where = lanes(c * chunk, chunk)
         return pltpu.make_async_remote_copy(
-            src_ref=sbuf.at[zz, :, where],
-            dst_ref=(low if up else high).at[zz, :, where],
+            src_ref=code.at[zz, c],
+            dst_ref=(low if up else high).at[zz, c],
             send_sem=z_send.at[zz, c],
             recv_sem=(low_recv if up else high_recv).at[zz, c],
             device_id=at_dp(z + 1 if up else z - 1, x),
             device_id_type=MESH,
         )
 
-    def sum_block(zz, where, extras):
+    def sum_block(zz, c, b, extras):
+        where = lanes(c * chunk + b * BLOCK, BLOCK)
         total = own[zz, :, where].astype(F32)
         for k in range(1, X):
             total = total + xr[zz, k - 1, :, where].astype(F32)
         for r in extras:
-            total = total + r[zz, :, where]
+            total = total + decode(r[zz, c, :, lanes(b * BLOCK, BLOCK)], r[zz, c, :, pl.ds(chunk, 128)])
         return total
 
     def add_chunk(zz, c, extras):
-        def body(b, carry):
-            where = lanes(c * chunk + b * BLOCK, BLOCK)
-            sbuf[zz, :, where] = sum_block(zz, where, extras)
+        def add(b, peak):
+            total = sum_block(zz, c, b, extras)
+            exact[:, lanes(b * BLOCK, BLOCK)] = total
+            return jnp.maximum(peak, lane_peak(total))
+
+        peak = lax.fori_loop(0, chunk // BLOCK, add, jnp.zeros((own.shape[1], 128), F32))
+        peak = (jnp.maximum(peak, TINY) * 1.01).astype(jnp.bfloat16)
+        code[zz, c, :, pl.ds(chunk, 128)] = peak
+        scale = spread_lanes(SPAN / peak.astype(F32))
+
+        def write(b, carry):
+            where = lanes(b * BLOCK, BLOCK)
+            code[zz, c, :, where] = encode(exact[:, where], scale)
             return carry
 
-        lax.fori_loop(0, chunk // BLOCK, body, 0)
+        lax.fori_loop(0, chunk // BLOCK, write, 0)
 
     def hop(zz, c, up):
         for k in range(1, X):
@@ -171,9 +206,8 @@
 
     def finish_chunk(c, extras):
         def body(b, carry):
-            where = lanes(c * chunk + b * BLOCK, BLOCK)
-            mean = sum_block(z, where, extras) / n
-            sbuf[z, :, where] = mean
+            mean = sum_block(z, c, b, extras) / n
+            mean_grad[:, lanes(c * chunk + b * BLOCK, BLOCK)] = mean
             return carry + mean * mean
 
         squares = lax.fori_loop(0, chunk // BLOCK, body, jnp.zeros((own.shape[1], BLOCK), F32))
@@ -280,7 +314,7 @@
         def body(b, inner):
             where = lanes(c * chunk + b * BLOCK, BLOCK)
             m, f, s = adam_update(
-                sbuf[z, :, where], master[:, where], first[:, where], second[:, where], clip_factor
+                mean_grad[:, where], master[:, where], first[:, where], second[:, where], clip_factor
             )
             master[:, where] = m
             first[:, where] = f
@@ -421,7 +455,7 @@
     shapes = (jax.ShapeDtypeStruct((layers, flat), jnp.bfloat16), piece, piece, piece)
     arrays = (local_grads[0, 0], master_weights[0], first_moment[0], second_moment[0])
     out_bytes = layers * (2 * flat + 3 * 4 * share)
-    used_bytes = layers * Z * share * (2 * X + 3 * 4) + out_bytes
+    used_bytes = layers * Z * share * (2 * X + 3 * 2) + layers * share * 4 + out_bytes
     results = pl.pallas_call(
         functools.partial(kernel, Z, X, E, share),
         out_shape=shapes,
@@ -430,9 +464,11 @@
         scratch_shapes=[
             pltpu.VMEM((Z, layers, share), jnp.bfloat16),
             pltpu.VMEM((Z, X - 1, layers, share), jnp.bfloat16),
-            pltpu.VMEM((Z, layers, share), F32),
-            pltpu.VMEM((Z, layers, share), F32),
-            pltpu.VMEM((Z, layers, share), F32),
+            pltpu.VMEM((Z, CHUNKS, layers, share // CHUNKS + 128), jnp.bfloat16),
+            pltpu.VMEM((Z, CHUNKS, layers, share // CHUNKS + 128), jnp.bfloat16),
+            pltpu.VMEM((Z, CHUNKS, layers, share // CHUNKS + 128), jnp.bfloat16),
+            pltpu.VMEM((layers, share // CHUNKS), F32),
+            pltpu.VMEM((layers, share), F32),
             pltpu.VMEM((n, 8, 128), F32),
             pltpu.VMEM((E, 8, 128), F32),
             dma((Z,)), dma((3,)),

time: 136 us -> 111 us (0.82)
  Pallas kernels: 135 us -> 110 us
    pallas_call x1, Pallas kernels: 132 us -> 107 us  [shards(): pl.pallas_call(functools.partial(kernel, Z, X, E, share), out_shape=shape...]
where the time goes in v1:
time: 111 us
  Pallas kernels  110 us (99%)
    pallas_call x1, Pallas kernels, shards(): pl.pallas_call(functools.partial(kernel, Z, X, E, share), out_shape=shape...  107 us
    pallas_call x1, Pallas kernels, shards(): pl.pallas_call(functools.partial(write_out, len(shapes)), out_shape=shape...  3.22 us

profile of v1, /device:TPU:0, one launch (start us, length us, event | category | flops | bytes accessed | tf_op | source)
XLA Modules:
  0.0 111.1 jit_solution(15349898832124760942)
XLA Ops:
  0.6 107.3 %shard_map.75 = (bf16[4,524288]{1,0:T(4,128)(2,1)S(1)}, f32[4,65536]{1,0:T(4,128)S(1)}, f32[4,65536]{1,0:T(4,128)S(1)}, f32[4,65536]{1,0:T(4,128)S(1)}) custom-call(bf16[4,524288]{1,0:T(4,128)(2,1)} %bitcast.8, f32[4,65536]{1,0:T(4,128)} %bitcast.9, f32[4,65536]{1,0:T(4,128)} %bitcast.10, f32[4,65536]{1,0:T(4,128)} %bitcast.11), custom_call_target="tpu_custom_call" | custom-call | tf_op jit(solution)/shard_map/pallas_call | solution.py:459
  107.9 3.2 %shard_map.76 = (bf16[4,524288]{1,0:T(4,128)(2,1)}, f32[4,65536]{1,0:T(4,128)}, f32[4,65536]{1,0:T(4,128)}, f32[4,65536]{1,0:T(4,128)}) custom-call(bf16[4,524288]{1,0:T(4,128)(2,1)S(1)} %get-tuple-element.12.refs_0_, f32[4,65536]{1,0:T(4,128)S(1)} %get-tuple-element.13.refs_1_, f32[4,65536]{1,0:T(4,128)S(1)} %get-tuple-element.14.refs_2_, ...), custom_call_target="tpu_custom_call" | custom-call | tf_op jit(solution)/shard_map/pallas_call | solution.py:484

commit v2 on v1

--- a/solution.py
+++ b/solution.py
@@ -64,8 +64,9 @@
     Z, X, E, share,
     grads, master_in, first_in, second_in,
     gathered, master, first, second,
-    own, xr, low, high, code, exact, mean_grad, norms, norms2,
-    own_sem, state_sem, x_send, x_recv, z_send, low_recv, high_recv,
+    own, side, xr, pr, xc, raw, chain, code, xcode, exact, mean_grad, norms, norms2,
+    own_sem, state_sem, x_send, x_recv, z_send, z_recv,
+    p_send, p_recv, q_send, q_recv, r_send, r_recv,
     n_send, n_recv, m_send, m_recv, g_send, g_recv, h_send,
 ):
     n = Z * X
@@ -80,17 +81,45 @@
     def lanes(base, size):
         return pl.ds(pl.multiple_of(base, 128), size)
 
-    barrier = pltpu.get_barrier_semaphore()
-    for k in range(1, n):
-        pl.semaphore_signal(barrier, inc=1, device_id=((dp + k) % n, ex), device_id_type=MESH)
-    for k in range(1, E):
-        pl.semaphore_signal(barrier, inc=1, device_id=(dp, (ex + k) % E), device_id_type=MESH)
-    pl.semaphore_wait(barrier, n - 1 + E - 1)
+    pair = z + 1 - 2 * (z % 2)
+    edge = jnp.logical_or(z == 0, z == Z - 1)
+    inside = jnp.logical_not(edge)
 
     def own_copy(zz):
         return pltpu.make_async_copy(
             grads.at[:, lanes((zz * X + x) * share, share)], own.at[zz], own_sem.at[zz]
         )
+
+    def side_copy(k):
+        start = (z * X + (x + k) % X) * share + HALF * chunk
+        return pltpu.make_async_copy(
+            grads.at[:, lanes(start, HALF * chunk)], side.at[k - 1], own_sem.at[Z + k - 1]
+        )
+
+    states = [
+        pltpu.make_async_copy(a, b, state_sem.at[i])
+        for i, (a, b) in enumerate(((master_in, master), (first_in, first), (second_in, second)))
+    ]
+
+    barrier = pltpu.get_barrier_semaphore()
+
+    def greet(device):
+        pl.semaphore_signal(barrier, inc=1, device_id=device, device_id_type=MESH)
+
+    for k in range(1, X):
+        greet(at_dp(z, (x + k) % X))
+    for k in range(1, E):
+        greet((dp, (ex + k) % E))
+
+    @pl.when(z > 0)
+    def _():
+        greet(at_dp(z - 1, x))
+
+    @pl.when(z < Z - 1)
+    def _():
+        greet(at_dp(z + 1, x))
+
+    pl.semaphore_wait(barrier, X + E - jnp.where(edge, 1, 0))
 
     def x_copy(zz, k, c):
         to = (x + k) % X
@@ -103,6 +132,57 @@
             device_id_type=MESH,
         )
 
+    def p_copy(k, c):
+        return pltpu.make_async_remote_copy(
+            src_ref=grads.at[:, lanes((pair * X + (x + k) % X) * share + c * chunk, chunk)],
+            dst_ref=pr.at[k - 1, :, lanes((c - HALF) * chunk, chunk)],
+            send_sem=p_send.at[k - 1, c - HALF],
+            recv_sem=p_recv.at[k - 1, c - HALF],
+            device_id=at_dp(pair, x),
+            device_id_type=MESH,
+        )
+
+    def q_copy(k, c):
+        return pltpu.make_async_remote_copy(
+            src_ref=xcode.at[k - 1, c - HALF],
+            dst_ref=xc.at[k - 1, c - HALF],
+            send_sem=q_send.at[k - 1, c - HALF],
+            recv_sem=q_recv.at[k - 1, c - HALF],
+            device_id=at_dp(z, (x + k) % X),
+            device_id_type=MESH,
+        )
+
+    def r_copy(c):
+        return pltpu.make_async_remote_copy(
+            src_ref=grads.at[:, lanes((pair * X + x) * share + c * chunk, chunk)],
+            dst_ref=raw.at[:, lanes((c - HALF) * chunk, chunk)],
+            send_sem=r_send.at[c - HALF],
+            recv_sem=r_recv.at[c - HALF],
+            device_id=at_dp(pair, x),
+            device_id_type=MESH,
+        )
+
+    def z_copy(zz, c):
+        up = jnp.where(zz > z, 1, 0)
+        return pltpu.make_async_remote_copy(
+            src_ref=code.at[zz, c],
+            dst_ref=chain.at[up, zz, c],
+            send_sem=z_send.at[zz, c],
+            recv_sem=z_recv.at[up, zz, c],
+            device_id=at_dp(z - 1 + 2 * up, x),
+            device_id_type=MESH,
+        )
+
+    def from_chain(up, zz, c):
+        return pltpu.make_async_remote_copy(
+            src_ref=code.at[zz, c],
+            dst_ref=chain.at[up, zz, c],
+            send_sem=z_send.at[zz, c],
+            recv_sem=z_recv.at[up, zz, c],
+            device_id=at_dp(z, (x + 1) % X),
+            device_id_type=MESH,
+        )
+
     def for_dest(k, act):
         @pl.when(z + k < Z)
         def _():
@@ -115,131 +195,206 @@
 
     def start_first(zz):
         own_copy(zz).start()
+        near = jnp.logical_or(zz == z, zz == pair)
 
         def body(c, carry):
             for k in range(1, X):
                 x_copy(zz, k, c).start()
             return carry
 
-        lax.fori_loop(0, CHUNKS, body, 0)
+        lax.fori_loop(0, jnp.where(near, HALF, CHUNKS), body, 0)
+
+    def over_late(act):
+        def body(c, carry):
+            act(c)
+            return carry
+
+        lax.fori_loop(HALF, CHUNKS, body, 0)
+
+    @over_late
+    def _(c):
+        for k in range(1, X):
+            p_copy(k, c).start()
 
     for k in range(Z - 1, -1, -1):
         for_dest(k, start_first)
-    states = [
-        pltpu.make_async_copy(a, b, state_sem.at[i])
-        for i, (a, b) in enumerate(((master_in, master), (first_in, first), (second_in, second)))
-    ]
+    for k in range(1, X):
+        side_copy(k).start()
     for s in states:
         s.start()
 
-    def z_copy(zz, c, up):
-        return pltpu.make_async_remote_copy(
-            src_ref=code.at[zz, c],
-            dst_ref=(low if up else high).at[zz, c],
-            send_sem=z_send.at[zz, c],
-            recv_sem=(low_recv if up else high_recv).at[zz, c],
-            device_id=at_dp(z + 1 if up else z - 1, x),
-            device_id_type=MESH,
-        )
-
-    def sum_block(zz, c, b, extras):
-        where = lanes(c * chunk + b * BLOCK, BLOCK)
-        total = own[zz, :, where].astype(F32)
-        for k in range(1, X):
-            total = total + xr[zz, k - 1, :, where].astype(F32)
-        for r in extras:
-            total = total + decode(r[zz, c, :, lanes(b * BLOCK, BLOCK)], r[zz, c, :, pl.ds(chunk, 128)])
-        return total
-
-    def add_chunk(zz, c, extras):
+    def part(ref, c, b):
+        return ref[:, lanes(c * chunk + b * BLOCK, BLOCK)].astype(F32)
+
+    def unpack(ref, b):
+        return decode(ref[:, lanes(b * BLOCK, BLOCK)], ref[:, pl.ds(chunk, 128)])
+
+    def pack(ref, block_sum):
         def add(b, peak):
-            total = sum_block(zz, c, b, extras)
+            total = block_sum(b)
             exact[:, lanes(b * BLOCK, BLOCK)] = total
             return jnp.maximum(peak, lane_peak(total))
 
         peak = lax.fori_loop(0, chunk // BLOCK, add, jnp.zeros((own.shape[1], 128), F32))
         peak = (jnp.maximum(peak, TINY) * 1.01).astype(jnp.bfloat16)
-        code[zz, c, :, pl.ds(chunk, 128)] = peak
+        ref[:, pl.ds(chunk, 128)] = peak
         scale = spread_lanes(SPAN / peak.astype(F32))
 
         def write(b, carry):
             where = lanes(b * BLOCK, BLOCK)
-            code[zz, c, :, where] = encode(exact[:, where], scale)
+            ref[:, where] = encode(exact[:, where], scale)
             return carry
 
         lax.fori_loop(0, chunk // BLOCK, write, 0)
 
-    def hop(zz, c, up):
-        for k in range(1, X):
-            x_copy(zz, k, c).wait_recv()
-        edge = z == (0 if up else Z - 1)
-
-        @pl.when(edge)
-        def _():
-            add_chunk(zz, c, ())
-
-        @pl.when(jnp.logical_not(edge))
-        def _():
-            z_copy(zz, c, up).wait_recv()
-            add_chunk(zz, c, (low if up else high,))
-
-        z_copy(zz, c, up).start()
+    def gather_sum(zz, c, with_x, ups):
+        def block_sum(b):
+            total = part(own.at[zz], c, b)
+            if with_x:
+                for k in range(1, X):
+                    total = total + part(xr.at[zz, k - 1], c, b)
+            for up in ups:
+                total = total + unpack(chain.at[up, zz, c], b)
+            return total
+
+        return block_sum
+
+    def hop(zz, c):
+        late = jnp.logical_and(zz == pair, c >= HALF)
+        up = jnp.where(zz > z, 1, 0)
+        first = z == (1 - up) * (Z - 1)
+        later = jnp.logical_not(first)
+
+        @pl.when(jnp.logical_not(late))
+        def _():
+            for k in range(1, X):
+                x_copy(zz, k, c).wait_recv()
+
+        @pl.when(later)
+        def _():
+            from_chain(up, zz, c).wait_recv()
+
+        @pl.when(jnp.logical_and(first, jnp.logical_not(late)))
+        def _():
+            pack(code.at[zz, c], gather_sum(zz, c, True, ()))
+
+        @pl.when(jnp.logical_and(later, jnp.logical_not(late)))
+        def _():
+            pack(code.at[zz, c], gather_sum(zz, c, True, (up,)))
+
+        @pl.when(jnp.logical_and(later, late))
+        def _():
+            pack(code.at[zz, c], gather_sum(zz, c, False, (up,)))
+
+        @pl.when(jnp.logical_not(jnp.logical_and(first, late)))
+        def _():
+            z_copy(zz, c).start()
 
     for k in range(Z - 1, 0, -1):
         for_dest(k, lambda zz: own_copy(zz).wait())
-
-        def body(c, carry, k=k):
-            @pl.when(z + k < Z)
-            def _():
-                hop(z + k, c, True)
-
-            @pl.when(z - k >= 0)
-            def _():
-                hop(z - k, c, False)
-
+        lower, upper = z - k >= 0, z + k < Z
+        count = jnp.where(lower, 1, 0) + jnp.where(upper, 1, 0)
+
+        def body(i, carry, k=k, upper=upper, count=count):
+            goes_up = jnp.logical_and(upper, i % count == 0)
+            hop(jnp.where(goes_up, z + k, z - k), i // count)
             return carry
 
-        lax.fori_loop(0, CHUNKS, body, 0)
+        @pl.when(count > 0)
+        def _(body=body, count=count):
+            lax.fori_loop(0, CHUNKS * count, body, 0)
+
+        if k == Z - 1:
+            @pl.when(edge)
+            def _():
+                over_late(lambda c: r_copy(c).start())
+
+            for j in range(1, X):
+                side_copy(j).wait()
+
+            @over_late
+            def _(c):
+                for j in range(1, X):
+                    p_copy(j, c).wait_recv()
+                    pack(
+                        xcode.at[j - 1, c - HALF],
+                        lambda b: part(side.at[j - 1], c - HALF, b) + part(pr.at[j - 1], c - HALF, b),
+                    )
+                    q_copy(j, c).start()
 
     own_copy(z).wait()
     norms2[0] = jnp.zeros((8, 128), F32)
 
-    def finish_chunk(c, extras):
+    def finish_chunk(c, block_sum):
         def body(b, carry):
-            mean = sum_block(z, c, b, extras) / n
+            mean = block_sum(b) / n
             mean_grad[:, lanes(c * chunk + b * BLOCK, BLOCK)] = mean
             return carry + mean * mean
 
         squares = lax.fori_loop(0, chunk // BLOCK, body, jnp.zeros((own.shape[1], BLOCK), F32))
         norms2[0] = norms2[0] + jnp.full((8, 128), jnp.sum(squares), F32)
 
-    def finish(c, carry):
+    def late_sum(c, ups, with_raw):
+        chained = gather_sum(z, c, False, ups)
+
+        def block_sum(b):
+            total = chained(b)
+            for k in range(1, X):
+                total = total + unpack(xc.at[k - 1, c - HALF], b)
+            if with_raw:
+                total = total + part(raw, c - HALF, b)
+            return total
+
+        return block_sum
+
+    far = jnp.where(pair < z, 0, 1)
+    far = jnp.where(edge, jnp.where(z == 0, 0, 1), far)
+    raw_pair = jnp.logical_and(inside, jnp.logical_or(pair == 0, pair == Z - 1))
+    both_pair = jnp.logical_and(inside, jnp.logical_not(raw_pair))
+
+    def early_finish(c):
         for k in range(1, X):
             x_copy(z, k, c).wait_recv()
 
-        @pl.when(z > 0)
-        def _():
-            z_copy(z, c, True).wait_recv()
-
-        @pl.when(z < Z - 1)
-        def _():
-            z_copy(z, c, False).wait_recv()
-
-        @pl.when(z == 0)
-        def _():
-            finish_chunk(c, (high,))
-
-        @pl.when(z == Z - 1)
-        def _():
-            finish_chunk(c, (low,))
-
-        @pl.when(jnp.logical_and(z > 0, z < Z - 1))
-        def _():
-            finish_chunk(c, (low, high))
-
+        @pl.when(edge)
+        def _():
+            from_chain(far, z, c).wait_recv()
+            finish_chunk(c, gather_sum(z, c, True, (far,)))
+
+        @pl.when(inside)
+        def _():
+            for up in range(2):
+                from_chain(up, z, c).wait_recv()
+            finish_chunk(c, gather_sum(z, c, True, (0, 1)))
+
+    def late_finish(c):
+        for k in range(1, X):
+            q_copy(k, c).wait_recv()
+
+        @pl.when(edge)
+        def _():
+            from_chain(far, z, c).wait_recv()
+            finish_chunk(c, late_sum(c, (far,), False))
+
+        @pl.when(raw_pair)
+        def _():
+            from_chain(far, z, c).wait_recv()
+            r_copy(c).wait_recv()
+            finish_chunk(c, late_sum(c, (far,), True))
+
+        if Z > 4:
+            @pl.when(both_pair)
+            def _():
+                for up in range(2):
+                    from_chain(up, z, c).wait_recv()
+                finish_chunk(c, late_sum(c, (0, 1), False))
+
+    def finish(c, carry):
+        early_finish(c)
+        late_finish(c + HALF)
         return carry
 
-    lax.fori_loop(0, CHUNKS, finish, 0)
+    lax.fori_loop(0, HALF, finish, 0)
 
     norms[0] = norms2[0]
 
@@ -294,8 +449,6 @@
             device_id=(dp, (ex + 1) % E), device_id_type=MESH,
         ).wait_recv()
 
-    pair = z + 1 - 2 * (z % 2)
-
     def h_copy(k, c):
         where = lanes((z * X + (x + k) % X) * share + c * chunk, chunk)
         return pltpu.make_async_remote_copy(
@@ -386,17 +539,19 @@
 
     def drain(c, carry):
         for zz in range(Z):
-            for k in range(1, X):
-                x_copy(zz, k, c).wait_send()
+            near = jnp.logical_or(zz == z, zz == pair)
+
+            @pl.when(jnp.logical_not(jnp.logical_and(near, c >= HALF)))
+            def _():
+                for k in range(1, X):
+                    x_copy(zz, k, c).wait_send()
+
             along_x(zz, c, lambda copy: copy.wait_send())
-
-            @pl.when(zz > z)
-            def _():
-                z_copy(zz, c, True).wait_send()
-
-            @pl.when(zz < z)
-            def _():
-                z_copy(zz, c, False).wait_send()
+            direct = jnp.logical_and(jnp.logical_and(edge, zz == pair), c >= HALF)
+
+            @pl.when(jnp.logical_and(zz != z, jnp.logical_not(direct)))
+            def _():
+                z_copy(zz, c).wait_send()
 
             @pl.when(jnp.logical_and(zz <= z, z < Z - 1))
             def _():
@@ -410,6 +565,12 @@
         def _():
             for k in range(1, X):
                 h_copy(k, c).wait_send()
+                p_copy(k, c).wait_send()
+                q_copy(k, c).wait_send()
+
+        @pl.when(jnp.logical_and(c >= HALF, edge))
+        def _():
+            r_copy(c).wait_send()
 
         return carry
 
@@ -455,7 +616,8 @@
     shapes = (jax.ShapeDtypeStruct((layers, flat), jnp.bfloat16), piece, piece, piece)
     arrays = (local_grads[0, 0], master_weights[0], first_moment[0], second_moment[0])
     out_bytes = layers * (2 * flat + 3 * 4 * share)
-    used_bytes = layers * Z * share * (2 * X + 3 * 2) + layers * share * 4 + out_bytes
+    coded = share // CHUNKS + 128
+    used_bytes = layers * share * (Z * (2 * X + 3 * 2) + 4 * X + 5) + out_bytes
     results = pl.pallas_call(
         functools.partial(kernel, Z, X, E, share),
         out_shape=shapes,
@@ -463,17 +625,23 @@
         out_specs=(local,) * 4,
         scratch_shapes=[
             pltpu.VMEM((Z, layers, share), jnp.bfloat16),
+            pltpu.VMEM((X - 1, layers, share // 2), jnp.bfloat16),
             pltpu.VMEM((Z, X - 1, layers, share), jnp.bfloat16),
-            pltpu.VMEM((Z, CHUNKS, layers, share // CHUNKS + 128), jnp.bfloat16),
-            pltpu.VMEM((Z, CHUNKS, layers, share // CHUNKS + 128), jnp.bfloat16),
-            pltpu.VMEM((Z, CHUNKS, layers, share // CHUNKS + 128), jnp.bfloat16),
+            pltpu.VMEM((X - 1, layers, share // 2), jnp.bfloat16),
+            pltpu.VMEM((X - 1, HALF, layers, coded), jnp.bfloat16),
+            pltpu.VMEM((layers, share // 2), jnp.bfloat16),
+            pltpu.VMEM((2, Z, CHUNKS, layers, coded), jnp.bfloat16),
+            pltpu.VMEM((Z, CHUNKS, layers, coded), jnp.bfloat16),
+            pltpu.VMEM((X - 1, HALF, layers, coded), jnp.bfloat16),
             pltpu.VMEM((layers, share // CHUNKS), F32),
             pltpu.VMEM((layers, share), F32),
             pltpu.VMEM((n, 8, 128), F32),
             pltpu.VMEM((E, 8, 128), F32),
-            dma((Z,)), dma((3,)),
+            dma((Z + X - 1,)), dma((3,)),
             dma((Z, X - 1, CHUNKS)), dma((Z, X - 1, CHUNKS)),
-            dma((Z, CHUNKS)), dma((Z, CHUNKS)), dma((Z, CHUNKS)),
+            dma((Z, CHUNKS)), dma((2, Z, CHUNKS)),
+            dma((X - 1, HALF)), dma((X - 1, HALF)), dma((X - 1, HALF)), dma((X - 1, HALF)),
+            dma((HALF,)), dma((HALF,)),
             dma((n,)), dma((n,)), dma((E,)), dma((E,)),
             dma((X + 1, Z, CHUNKS)), dma((n, CHUNKS)), dma((X - 1, CHUNKS)),
         ],

time: 111 us -> 106 us (0.955)
  Pallas kernels: 110 us -> 105 us
    pallas_call x1, Pallas kernels: 107 us -> 102 us  [shards(): pl.pallas_call(functools.partial(kernel, Z, X, E, share), out_shape=shape...]
where the time goes in v2:
time: 106 us
  Pallas kernels  105 us (99%)
    pallas_call x1, Pallas kernels, shards(): pl.pallas_call(functools.partial(kernel, Z, X, E, share), out_shape=shape...  102 us
    pallas_call x1, Pallas kernels, shards(): pl.pallas_call(functools.partial(write_out, len(shapes)), out_shape=shape...  3.22 us

profile of v2, /device:TPU:0, one launch (start us, length us, event | category | flops | bytes accessed | tf_op | source)
XLA Modules:
  0.0 105.9 jit_solution(3470377460530532660)
XLA Ops:
  0.6 102.1 %shard_map.75 = (bf16[4,524288]{1,0:T(4,128)(2,1)S(1)}, f32[4,65536]{1,0:T(4,128)S(1)}, f32[4,65536]{1,0:T(4,128)S(1)}, f32[4,65536]{1,0:T(4,128)S(1)}) custom-call(bf16[4,524288]{1,0:T(4,128)(2,1)} %bitcast.8, f32[4,65536]{1,0:T(4,128)} %bitcast.9, f32[4,65536]{1,0:T(4,128)} %bitcast.10, f32[4,65536]{1,0:T(4,128)} %bitcast.11), custom_call_target="tpu_custom_call" | custom-call | tf_op jit(solution)/shard_map/pallas_call | solution.py:621
  102.7 3.2 %shard_map.76 = (bf16[4,524288]{1,0:T(4,128)(2,1)}, f32[4,65536]{1,0:T(4,128)}, f32[4,65536]{1,0:T(4,128)}, f32[4,65536]{1,0:T(4,128)}) custom-call(bf16[4,524288]{1,0:T(4,128)(2,1)S(1)} %get-tuple-element.12.refs_0_, f32[4,65536]{1,0:T(4,128)S(1)} %get-tuple-element.13.refs_1_, f32[4,65536]{1,0:T(4,128)S(1)} %get-tuple-element.14.refs_2_, ...), custom_call_target="tpu_custom_call" | custom-call | tf_op jit(solution)/shard_map/pallas_call | solution.py:652

commit v3 on v2

--- a/solution.py
+++ b/solution.py
@@ -19,8 +19,10 @@
 
 MESH = pl.DeviceIdType.MESH
 F32 = jnp.float32
-CHUNKS = 8
+CHUNKS = 4
 HALF = CHUNKS // 2
+SENDS = 4
+SEND_HALF = SENDS // 2
 PIECES = 8
 SPARE_BYTES = 4 * 1024 * 1024
 BLOCK = 2048
@@ -64,16 +66,17 @@
     Z, X, E, share,
     grads, master_in, first_in, second_in,
     gathered, master, first, second,
-    own, side, xr, pr, xc, raw, chain, code, xcode, exact, mean_grad, norms, norms2,
+    own, side, xr, pr, xc, raw, chain, code, xcode, exact, mean_grad, squares, norms,
     own_sem, state_sem, x_send, x_recv, z_send, z_recv,
     p_send, p_recv, q_send, q_recv, r_send, r_recv,
-    n_send, n_recv, m_send, m_recv, g_send, g_recv, h_send,
+    n_send, n_recv, g_send, g_recv, h_send,
 ):
     n = Z * X
     dp = lax.axis_index("dp")
     ex = lax.axis_index("expert")
     z, x = dp // X, dp % X
     chunk = share // CHUNKS
+    piece = share // SENDS
 
     def at_dp(zz, xx):
         return (zz * X + xx, ex)
@@ -323,7 +326,7 @@
                     q_copy(j, c).start()
 
     own_copy(z).wait()
-    norms2[0] = jnp.zeros((8, 128), F32)
+    squares[...] = jnp.zeros_like(squares)
 
     def finish_chunk(c, block_sum):
         def body(b, carry):
@@ -331,8 +334,7 @@
             mean_grad[:, lanes(c * chunk + b * BLOCK, BLOCK)] = mean
             return carry + mean * mean
 
-        squares = lax.fori_loop(0, chunk // BLOCK, body, jnp.zeros((own.shape[1], BLOCK), F32))
-        norms2[0] = norms2[0] + jnp.full((8, 128), jnp.sum(squares), F32)
+        squares[...] = lax.fori_loop(0, chunk // BLOCK, body, squares[...])
 
     def late_sum(c, ups, with_raw):
         chained = gather_sum(z, c, False, ups)
@@ -396,41 +398,38 @@
 
     lax.fori_loop(0, HALF, finish, 0)
 
-    norms[0] = norms2[0]
+    sums = squares[...]
+    while sums.shape[1] > 128:
+        half = sums.shape[1] // 2
+        sums = sums[:, :half] + sums[:, half:]
+    norms[0] = jnp.sum(sums, axis=0, keepdims=True)
+    everyone = n * E
 
     def n_copy(k):
+        to = (dp * E + ex + k) % everyone
         return pltpu.make_async_remote_copy(
             src_ref=norms.at[0], dst_ref=norms.at[k],
             send_sem=n_send.at[k], recv_sem=n_recv.at[k],
-            device_id=((dp + k) % n, ex), device_id_type=MESH,
-        )
-
-    def m_copy(k):
-        return pltpu.make_async_remote_copy(
-            src_ref=norms2.at[0], dst_ref=norms2.at[k],
-            send_sem=m_send.at[k], recv_sem=m_recv.at[k],
-            device_id=(dp, (ex + k) % E), device_id_type=MESH,
-        )
-
-    for k in range(1, n):
-        n_copy(k).start()
+            device_id=(to // E, to % E), device_id_type=MESH,
+        )
+
+    def over_others(act):
+        def body(k, carry):
+            act(k)
+            return carry
+
+        lax.fori_loop(1, everyone, body, 0)
+
+    over_others(lambda k: n_copy(k).start())
     for s in states:
         s.wait()
-    total = norms[0]
-    for k in range(1, n):
-        n_copy(k).wait_recv()
-        total = total + norms[k]
-    norms2[0] = total
-    for k in range(1, E):
-        m_copy(k).start()
-    for k in range(1, E):
-        m_copy(k).wait_recv()
-        total = total + norms2[k]
+    over_others(lambda k: n_copy(k).wait_recv())
+    total = jnp.full((8, 128), jnp.sum(norms[...]), F32)
     clip_all = jnp.minimum(1.0, clip_limit / (jnp.sqrt(total) + norm_eps))
     clip_factor = jnp.max(clip_all)
 
     def g_copy(zz, c, way):
-        where = lanes((zz * X + x) * share + c * chunk, chunk)
+        where = lanes((zz * X + x) * share + c * piece, piece)
         if way < 2:
             target = at_dp(z + 1 if way == 0 else z - 1, x)
         else:
@@ -442,7 +441,7 @@
         )
 
     def arrived(zz, xx, c):
-        where = lanes((zz * X + xx) * share + c * chunk, chunk)
+        where = lanes((zz * X + xx) * share + c * piece, piece)
         pltpu.make_async_remote_copy(
             src_ref=gathered.at[:, where], dst_ref=gathered.at[:, where],
             send_sem=g_send.at[0, 0, c], recv_sem=g_recv.at[zz * X + xx, c],
@@ -450,7 +449,7 @@
         ).wait_recv()
 
     def h_copy(k, c):
-        where = lanes((z * X + (x + k) % X) * share + c * chunk, chunk)
+        where = lanes((z * X + (x + k) % X) * share + c * piece, piece)
         return pltpu.make_async_remote_copy(
             src_ref=gathered.at[:, where], dst_ref=gathered.at[:, where],
             send_sem=h_send.at[k - 1, c], recv_sem=g_recv.at[z * X + (x + k) % X, c],
@@ -458,24 +457,24 @@
         )
 
     def along_x(zz, c, act):
-        @pl.when(jnp.logical_or(zz != pair, c < HALF))
+        @pl.when(jnp.logical_or(zz != pair, c < SEND_HALF))
         def _():
             for k in range(1, X):
                 act(g_copy(zz, c, k + 1))
 
     def update(c, carry):
         def body(b, inner):
-            where = lanes(c * chunk + b * BLOCK, BLOCK)
+            where = lanes(c * piece + b * BLOCK, BLOCK)
             m, f, s = adam_update(
                 mean_grad[:, where], master[:, where], first[:, where], second[:, where], clip_factor
             )
             master[:, where] = m
             first[:, where] = f
             second[:, where] = s
-            gathered[:, lanes(dp * share + c * chunk + b * BLOCK, BLOCK)] = m.astype(jnp.bfloat16)
+            gathered[:, lanes(dp * share + c * piece + b * BLOCK, BLOCK)] = m.astype(jnp.bfloat16)
             return inner
 
-        lax.fori_loop(0, chunk // BLOCK, body, 0)
+        lax.fori_loop(0, piece // BLOCK, body, 0)
 
         @pl.when(z < Z - 1)
         def _():
@@ -489,7 +488,7 @@
             g_copy(z, c, k + 1).start()
         return carry
 
-    lax.fori_loop(0, CHUNKS, update, 0)
+    lax.fori_loop(0, SENDS, update, 0)
 
     for s in range(1, Z):
         def relay(c, carry, s=s):
@@ -515,16 +514,46 @@
 
             return carry
 
-        lax.fori_loop(0, CHUNKS, relay, 0)
-
-        if s == 1:
+        lax.fori_loop(0, SENDS, relay, 0)
+
+        if s == max(Z - 2, 1):
             def across(c, carry):
                 for k in range(1, X):
                     arrived(z, (x + k) % X, c)
                     h_copy(k, c).start()
                 return carry
 
-            lax.fori_loop(HALF, CHUNKS, across, 0)
+            lax.fori_loop(SEND_HALF, SENDS, across, 0)
+
+    def drain(c, carry):
+        for zz in range(Z):
+            near = jnp.logical_or(zz == z, zz == pair)
+
+            @pl.when(jnp.logical_not(jnp.logical_and(near, c >= HALF)))
+            def _():
+                for k in range(1, X):
+                    x_copy(zz, k, c).wait_send()
+
+            direct = jnp.logical_and(jnp.logical_and(edge, zz == pair), c >= HALF)
+
+            @pl.when(jnp.logical_and(zz != z, jnp.logical_not(direct)))
+            def _():
+                z_copy(zz, c).wait_send()
+
+        @pl.when(c >= HALF)
+        def _():
+            for k in range(1, X):
+                p_copy(k, c).wait_send()
+                q_copy(k, c).wait_send()
+
+        @pl.when(jnp.logical_and(c >= HALF, edge))
+        def _():
+            r_copy(c).wait_send()
+
+        return carry
+
+    lax.fori_loop(0, CHUNKS, drain, 0)
+    over_others(lambda k: n_copy(k).wait_send())
 
     for s in range(Z):
         def collect(zz, s=s):
@@ -533,25 +562,13 @@
                     arrived(zz, (x + k) % X, c)
                 return carry
 
-            lax.fori_loop(0, HALF if s == 0 else CHUNKS, body, 0)
+            lax.fori_loop(0, SEND_HALF if s == 0 else SENDS, body, 0)
 
         for_dest(s, collect)
 
-    def drain(c, carry):
+    def drain_sends(c, carry):
         for zz in range(Z):
-            near = jnp.logical_or(zz == z, zz == pair)
-
-            @pl.when(jnp.logical_not(jnp.logical_and(near, c >= HALF)))
-            def _():
-                for k in range(1, X):
-                    x_copy(zz, k, c).wait_send()
-
             along_x(zz, c, lambda copy: copy.wait_send())
-            direct = jnp.logical_and(jnp.logical_and(edge, zz == pair), c >= HALF)
-
-            @pl.when(jnp.logical_and(zz != z, jnp.logical_not(direct)))
-            def _():
-                z_copy(zz, c).wait_send()
 
             @pl.when(jnp.logical_and(zz <= z, z < Z - 1))
             def _():
@@ -561,24 +578,14 @@
             def _():
                 g_copy(zz, c, 1).wait_send()
 
-        @pl.when(c >= HALF)
+        @pl.when(c >= SEND_HALF)
         def _():
             for k in range(1, X):
                 h_copy(k, c).wait_send()
-                p_copy(k, c).wait_send()
-                q_copy(k, c).wait_send()
-
-        @pl.when(jnp.logical_and(c >= HALF, edge))
-        def _():
-            r_copy(c).wait_send()
 
         return carry
 
-    lax.fori_loop(0, CHUNKS, drain, 0)
-    for k in range(1, n):
-        n_copy(k).wait_send()
-    for k in range(1, E):
-        m_copy(k).wait_send()
+    lax.fori_loop(0, SENDS, drain_sends, 0)
 
 
 def write_out(count, *refs):
@@ -635,15 +642,15 @@
             pltpu.VMEM((X - 1, HALF, layers, coded), jnp.bfloat16),
             pltpu.VMEM((layers, share // CHUNKS), F32),
             pltpu.VMEM((layers, share), F32),
-            pltpu.VMEM((n, 8, 128), F32),
-            pltpu.VMEM((E, 8, 128), F32),
+            pltpu.VMEM((layers, BLOCK), F32),
+            pltpu.VMEM((n * E, 1, 128), F32),
             dma((Z + X - 1,)), dma((3,)),
             dma((Z, X - 1, CHUNKS)), dma((Z, X - 1, CHUNKS)),
             dma((Z, CHUNKS)), dma((2, Z, CHUNKS)),
             dma((X - 1, HALF)), dma((X - 1, HALF)), dma((X - 1, HALF)), dma((X - 1, HALF)),
             dma((HALF,)), dma((HALF,)),
-            dma((n,)), dma((n,)), dma((E,)), dma((E,)),
-            dma((X + 1, Z, CHUNKS)), dma((n, CHUNKS)), dma((X - 1, CHUNKS)),
+            dma((n * E,)), dma((n * E,)),
+            dma((X + 1, Z, SENDS)), dma((n, SENDS)), dma((X - 1, SENDS)),
         ],
         compiler_params=pltpu.CompilerParams(
             collective_id=0, has_side_effects=True, vmem_limit_bytes=used_bytes + SPARE_BYTES

time: 106 us -> 99.4 us (0.938)
  Pallas kernels: 105 us -> 98.6 us
    pallas_call x1, Pallas kernels: 102 us -> 95.3 us  [shards(): pl.pallas_call(functools.partial(kernel, Z, X, E, share), out_shape=shape...]
where the time goes in v3:
time: 99.4 us; the launch traced here: 99.2 us
  Pallas kernels  98.6 us (99%)
    pallas_call x1, Pallas kernels, shards(): pl.pallas_call(functools.partial(kernel, Z, X, E, share), out_shape=shape...  95.3 us
    pallas_call x1, Pallas kernels, shards(): pl.pallas_call(functools.partial(write_out, len(shapes)), out_shape=shape...  3.22 us

profile of v3, /device:TPU:0, one launch (start us, length us, event | category | flops | bytes accessed | tf_op | source)
XLA Modules:
  0.0 99.2 jit_solution(14407503495924008704)
XLA Ops:
  0.6 95.3 %shard_map.75 = (bf16[4,524288]{1,0:T(4,128)(2,1)S(1)}, f32[4,65536]{1,0:T(4,128)S(1)}, f32[4,65536]{1,0:T(4,128)S(1)}, f32[4,65536]{1,0:T(4,128)S(1)}) custom-call(bf16[4,524288]{1,0:T(4,128)(2,1)} %bitcast.8, f32[4,65536]{1,0:T(4,128)} %bitcast.9, f32[4,65536]{1,0:T(4,128)} %bitcast.10, f32[4,65536]{1,0:T(4,128)} %bitcast.11), custom_call_target="tpu_custom_call" | custom-call | tf_op jit(solution)/shard_map/pallas_call | solution.py:628
  96.0 3.2 %shard_map.76 = (bf16[4,524288]{1,0:T(4,128)(2,1)}, f32[4,65536]{1,0:T(4,128)}, f32[4,65536]{1,0:T(4,128)}, f32[4,65536]{1,0:T(4,128)}) custom-call(bf16[4,524288]{1,0:T(4,128)(2,1)S(1)} %get-tuple-element.12.refs_0_, f32[4,65536]{1,0:T(4,128)S(1)} %get-tuple-element.13.refs_1_, f32[4,65536]{1,0:T(4,128)S(1)} %get-tuple-element.14.refs_2_, ...), custom_call_target="tpu_custom_call" | custom-call | tf_op jit(solution)/shard_map/pallas_call | solution.py:659

commit v4 on v3

--- a/solution.py
+++ b/solution.py
@@ -21,8 +21,7 @@
 F32 = jnp.float32
 CHUNKS = 4
 HALF = CHUNKS // 2
-SENDS = 4
-SEND_HALF = SENDS // 2
+CROSS = CHUNKS // 4
 PIECES = 8
 SPARE_BYTES = 4 * 1024 * 1024
 BLOCK = 2048
@@ -34,7 +33,7 @@
     scaled = clip_factor * gradient
     new_first = beta_first * first + (1.0 - beta_first) * scaled
     new_second = beta_second * second + (1.0 - beta_second) * scaled * scaled
-    direction = new_first / correct_first / (jnp.sqrt(new_second / correct_second) + tiny_eps)
+    direction = new_first * (1.0 / correct_first) / (jnp.sqrt(new_second * (1.0 / correct_second)) + tiny_eps)
     new_master = master - learn_rate * (decay_rate * master + direction)
     return (new_master, new_first, new_second)
 
@@ -66,17 +65,16 @@
     Z, X, E, share,
     grads, master_in, first_in, second_in,
     gathered, master, first, second,
-    own, side, xr, pr, xc, raw, chain, code, xcode, exact, mean_grad, squares, norms,
+    own, side, xr, pr, xc, raw, chain, code, xcode, exact, mean_grad, squares, norms, coded_state, coded_grad,
     own_sem, state_sem, x_send, x_recv, z_send, z_recv,
     p_send, p_recv, q_send, q_recv, r_send, r_recv,
-    n_send, n_recv, g_send, g_recv, h_send,
+    n_send, n_recv, s_send, s_recv, e_send, e_recv, g_send, g_recv, h_send,
 ):
     n = Z * X
     dp = lax.axis_index("dp")
     ex = lax.axis_index("expert")
     z, x = dp // X, dp % X
     chunk = share // CHUNKS
-    piece = share // SENDS
 
     def at_dp(zz, xx):
         return (zz * X + xx, ex)
@@ -87,6 +85,8 @@
     pair = z + 1 - 2 * (z % 2)
     edge = jnp.logical_or(z == 0, z == Z - 1)
     inside = jnp.logical_not(edge)
+    raw_pair = jnp.logical_and(inside, jnp.logical_or(pair == 0, pair == Z - 1))
+    both_pair = jnp.logical_and(inside, jnp.logical_not(raw_pair))
 
     def own_copy(zz):
         return pltpu.make_async_copy(
@@ -249,6 +249,33 @@
             return carry
 
         lax.fori_loop(0, chunk // BLOCK, write, 0)
+
+    def s_copy(j, i):
+        return pltpu.make_async_remote_copy(
+            src_ref=coded_state.at[j, i], dst_ref=coded_state.at[j, i],
+            send_sem=s_send.at[j, i], recv_sem=s_recv.at[j, i],
+            device_id=at_dp(pair, x), device_id_type=MESH,
+        )
+
+    def e_copy(i):
+        return pltpu.make_async_remote_copy(
+            src_ref=coded_grad.at[i], dst_ref=coded_grad.at[i],
+            send_sem=e_send.at[i], recv_sem=e_recv.at[i],
+            device_id=at_dp(pair, x), device_id_type=MESH,
+        )
+
+    for s in states:
+        s.wait()
+
+    @pl.when(raw_pair)
+    def _():
+        def send_state(i, carry):
+            for j, ref in enumerate((master, first, second)):
+                pack(coded_state.at[j, i], lambda b, ref=ref: part(ref, i * HALF, b))
+                s_copy(j, i).start()
+            return carry
+
+        lax.fori_loop(0, 2, send_state, 0)
 
     def gather_sum(zz, c, with_x, ups):
         def block_sum(b):
@@ -330,7 +357,7 @@
 
     def finish_chunk(c, block_sum):
         def body(b, carry):
-            mean = block_sum(b) / n
+            mean = block_sum(b) * (1.0 / n)
             mean_grad[:, lanes(c * chunk + b * BLOCK, BLOCK)] = mean
             return carry + mean * mean
 
@@ -351,9 +378,6 @@
 
     far = jnp.where(pair < z, 0, 1)
     far = jnp.where(edge, jnp.where(z == 0, 0, 1), far)
-    raw_pair = jnp.logical_and(inside, jnp.logical_or(pair == 0, pair == Z - 1))
-    both_pair = jnp.logical_and(inside, jnp.logical_not(raw_pair))
-
     def early_finish(c):
         for k in range(1, X):
             x_copy(z, k, c).wait_recv()
@@ -391,8 +415,15 @@
                     from_chain(up, z, c).wait_recv()
                 finish_chunk(c, late_sum(c, (0, 1), False))
 
+    def share_grad(i, now=True):
+        @pl.when(jnp.logical_and(raw_pair, now))
+        def _():
+            pack(coded_grad.at[i], lambda b: part(mean_grad, i * HALF, b))
+            e_copy(i).start()
+
     def finish(c, carry):
         early_finish(c)
+        share_grad(0, c == 0)
         late_finish(c + HALF)
         return carry
 
@@ -403,33 +434,33 @@
         half = sums.shape[1] // 2
         sums = sums[:, :half] + sums[:, half:]
     norms[0] = jnp.sum(sums, axis=0, keepdims=True)
-    everyone = n * E
-
-    def n_copy(k):
-        to = (dp * E + ex + k) % everyone
+    dp_at = [(dp + i) % n for i in range(n)]
+    ex_at = [(ex + j) % E for j in range(E)]
+    others = sorted(
+        [(i, j) for i in range(n) for j in range(E) if i + j], key=lambda o: min(o[0], n - o[0]), reverse=True
+    )
+
+    def n_copy(i, j):
+        k = i * E + j
         return pltpu.make_async_remote_copy(
             src_ref=norms.at[0], dst_ref=norms.at[k],
             send_sem=n_send.at[k], recv_sem=n_recv.at[k],
-            device_id=(to // E, to % E), device_id_type=MESH,
+            device_id=(dp_at[i], ex_at[j]), device_id_type=MESH,
         )
 
     def over_others(act):
-        def body(k, carry):
-            act(k)
-            return carry
-
-        lax.fori_loop(1, everyone, body, 0)
-
-    over_others(lambda k: n_copy(k).start())
-    for s in states:
-        s.wait()
-    over_others(lambda k: n_copy(k).wait_recv())
+        for i, j in others:
+            act(n_copy(i, j))
+
+    over_others(lambda copy: copy.start())
+    share_grad(1)
+    over_others(lambda copy: copy.wait_recv())
     total = jnp.full((8, 128), jnp.sum(norms[...]), F32)
     clip_all = jnp.minimum(1.0, clip_limit / (jnp.sqrt(total) + norm_eps))
     clip_factor = jnp.max(clip_all)
 
     def g_copy(zz, c, way):
-        where = lanes((zz * X + x) * share + c * piece, piece)
+        where = lanes((zz * X + x) * share + c * chunk, chunk)
         if way < 2:
             target = at_dp(z + 1 if way == 0 else z - 1, x)
         else:
@@ -441,7 +472,7 @@
         )
 
     def arrived(zz, xx, c):
-        where = lanes((zz * X + xx) * share + c * piece, piece)
+        where = lanes((zz * X + xx) * share + c * chunk, chunk)
         pltpu.make_async_remote_copy(
             src_ref=gathered.at[:, where], dst_ref=gathered.at[:, where],
             send_sem=g_send.at[0, 0, c], recv_sem=g_recv.at[zz * X + xx, c],
@@ -449,7 +480,7 @@
         ).wait_recv()
 
     def h_copy(k, c):
-        where = lanes((z * X + (x + k) % X) * share + c * piece, piece)
+        where = lanes((z * X + (x + k) % X) * share + c * chunk, chunk)
         return pltpu.make_async_remote_copy(
             src_ref=gathered.at[:, where], dst_ref=gathered.at[:, where],
             send_sem=h_send.at[k - 1, c], recv_sem=g_recv.at[z * X + (x + k) % X, c],
@@ -457,30 +488,74 @@
         )
 
     def along_x(zz, c, act):
-        @pl.when(jnp.logical_or(zz != pair, c < SEND_HALF))
+        @pl.when(jnp.logical_or(zz != pair, c < CROSS))
         def _():
             for k in range(1, X):
                 act(g_copy(zz, c, k + 1))
 
-    def update(c, carry):
+    def doubled(zz, c):
+        return jnp.logical_and(jnp.logical_and(edge, zz == pair), c % HALF == 0)
+
+    maker = jnp.where(edge, pair, z)
+
+    def make_params(i, carry):
         def body(b, inner):
-            where = lanes(c * piece + b * BLOCK, BLOCK)
+            m, f, s = (unpack(coded_state.at[j, i], b) for j in range(3))
+            m, f, s = adam_update(unpack(coded_grad.at[i], b), m, f, s, clip_factor)
+            start = (maker * X + x) * share + i * HALF * chunk + b * BLOCK
+            gathered[:, lanes(start, BLOCK)] = m.astype(jnp.bfloat16)
+            return inner
+
+        @pl.when(edge)
+        def _():
+            for j in range(3):
+                s_copy(j, i).wait_recv()
+            e_copy(i).wait_recv()
+
+        lax.fori_loop(0, chunk // BLOCK, body, 0)
+        return carry
+
+    def update_chunk(c, with_params):
+        def body(b, inner):
+            where = lanes(c * chunk + b * BLOCK, BLOCK)
             m, f, s = adam_update(
                 mean_grad[:, where], master[:, where], first[:, where], second[:, where], clip_factor
             )
             master[:, where] = m
             first[:, where] = f
             second[:, where] = s
-            gathered[:, lanes(dp * share + c * piece + b * BLOCK, BLOCK)] = m.astype(jnp.bfloat16)
+            if with_params:
+                gathered[:, lanes(dp * share + c * chunk + b * BLOCK, BLOCK)] = m.astype(jnp.bfloat16)
             return inner
 
-        lax.fori_loop(0, piece // BLOCK, body, 0)
-
-        @pl.when(z < Z - 1)
+        lax.fori_loop(0, chunk // BLOCK, body, 0)
+
+    rest = CHUNKS - 2
+
+    def in_turn(t):
+        return jnp.where(t < rest, t + 1 + jnp.where(t + 1 >= HALF, 1, 0), (t - rest) * HALF)
+
+    def update(t, carry):
+        c = in_turn(t)
+        made = jnp.logical_and(raw_pair, t >= rest)
+
+        @pl.when(jnp.logical_and(jnp.logical_not(both_pair), t == rest))
+        def _():
+            lax.fori_loop(0, 2, make_params, 0)
+
+        @pl.when(made)
+        def _():
+            update_chunk(c, False)
+
+        @pl.when(jnp.logical_not(made))
+        def _():
+            update_chunk(c, True)
+
+        @pl.when(jnp.logical_and(z < Z - 1, jnp.logical_not(jnp.logical_and(made, pair > z))))
         def _():
             g_copy(z, c, 0).start()
 
-        @pl.when(z > 0)
+        @pl.when(jnp.logical_and(z > 0, jnp.logical_not(jnp.logical_and(made, pair < z))))
         def _():
             g_copy(z, c, 1).start()
 
@@ -488,13 +563,17 @@
             g_copy(z, c, k + 1).start()
         return carry
 
-    lax.fori_loop(0, SENDS, update, 0)
+    lax.fori_loop(0, CHUNKS, update, 0)
 
     for s in range(1, Z):
-        def relay(c, carry, s=s):
+        def relay(t, carry, s=s):
+            c = in_turn(t)
+
             @pl.when(z - s >= 0)
             def _():
-                arrived(z - s, x, c)
+                @pl.when(jnp.logical_not(doubled(z - s, c)))
+                def _():
+                    arrived(z - s, x, c)
 
                 @pl.when(z < Z - 1)
                 def _():
@@ -504,7 +583,9 @@
 
             @pl.when(z + s < Z)
             def _():
-                arrived(z + s, x, c)
+                @pl.when(jnp.logical_not(doubled(z + s, c)))
+                def _():
+                    arrived(z + s, x, c)
 
                 @pl.when(z > 0)
                 def _():
@@ -514,7 +595,7 @@
 
             return carry
 
-        lax.fori_loop(0, SENDS, relay, 0)
+        lax.fori_loop(0, CHUNKS, relay, 0)
 
         if s == max(Z - 2, 1):
             def across(c, carry):
@@ -523,7 +604,7 @@
                     h_copy(k, c).start()
                 return carry
 
-            lax.fori_loop(SEND_HALF, SENDS, across, 0)
+            lax.fori_loop(CROSS, CHUNKS, across, 0)
 
     def drain(c, carry):
         for zz in range(Z):
@@ -553,7 +634,15 @@
         return carry
 
     lax.fori_loop(0, CHUNKS, drain, 0)
-    over_others(lambda k: n_copy(k).wait_send())
+
+    @pl.when(raw_pair)
+    def _():
+        for i in range(2):
+            for j in range(3):
+                s_copy(j, i).wait_send()
+            e_copy(i).wait_send()
+
+    over_others(lambda copy: copy.wait_send())
 
     for s in range(Z):
         def collect(zz, s=s):
@@ -562,7 +651,7 @@
                     arrived(zz, (x + k) % X, c)
                 return carry
 
-            lax.fori_loop(0, SEND_HALF if s == 0 else SENDS, body, 0)
+            lax.fori_loop(0, CROSS if s == 0 else CHUNKS, body, 0)
 
         for_dest(s, collect)
 
@@ -570,22 +659,25 @@
         for zz in range(Z):
             along_x(zz, c, lambda copy: copy.wait_send())
 
-            @pl.when(jnp.logical_and(zz <= z, z < Z - 1))
+            made = jnp.logical_and(jnp.logical_and(raw_pair, zz == z), c % HALF == 0)
+            no_up, no_down = jnp.logical_and(made, pair > z), jnp.logical_and(made, pair < z)
+
+            @pl.when(jnp.logical_and(jnp.logical_and(zz <= z, z < Z - 1), jnp.logical_not(no_up)))
             def _():
                 g_copy(zz, c, 0).wait_send()
 
-            @pl.when(jnp.logical_and(zz >= z, z > 0))
+            @pl.when(jnp.logical_and(jnp.logical_and(zz >= z, z > 0), jnp.logical_not(no_down)))
             def _():
                 g_copy(zz, c, 1).wait_send()
 
-        @pl.when(c >= SEND_HALF)
+        @pl.when(c >= CROSS)
         def _():
             for k in range(1, X):
                 h_copy(k, c).wait_send()
 
         return carry
 
-    lax.fori_loop(0, SENDS, drain_sends, 0)
+    lax.fori_loop(0, CHUNKS, drain_sends, 0)
 
 
 def write_out(count, *refs):
@@ -624,7 +716,7 @@
     arrays = (local_grads[0, 0], master_weights[0], first_moment[0], second_moment[0])
     out_bytes = layers * (2 * flat + 3 * 4 * share)
     coded = share // CHUNKS + 128
-    used_bytes = layers * share * (Z * (2 * X + 3 * 2) + 4 * X + 5) + out_bytes
+    used_bytes = layers * share * (Z * (2 * X + 3 * 2) + 4 * X + 9) + out_bytes
     results = pl.pallas_call(
         functools.partial(kernel, Z, X, E, share),
         out_shape=shapes,
@@ -644,13 +736,16 @@
             pltpu.VMEM((layers, share), F32),
             pltpu.VMEM((layers, BLOCK), F32),
             pltpu.VMEM((n * E, 1, 128), F32),
+            pltpu.VMEM((3, 2, layers, coded), jnp.bfloat16),
+            pltpu.VMEM((2, layers, coded), jnp.bfloat16),
             dma((Z + X - 1,)), dma((3,)),
             dma((Z, X - 1, CHUNKS)), dma((Z, X - 1, CHUNKS)),
             dma((Z, CHUNKS)), dma((2, Z, CHUNKS)),
             dma((X - 1, HALF)), dma((X - 1, HALF)), dma((X - 1, HALF)), dma((X - 1, HALF)),
             dma((HALF,)), dma((HALF,)),
             dma((n * E,)), dma((n * E,)),
-            dma((X + 1, Z, SENDS)), dma((n, SENDS)), dma((X - 1, SENDS)),
+            dma((3, 2)), dma((3, 2)), dma((2,)), dma((2,)),
+            dma((X + 1, Z, CHUNKS)), dma((n, CHUNKS)), dma((X - 1, CHUNKS)),
         ],
         compiler_params=pltpu.CompilerParams(
             collective_id=0, has_side_effects=True, vmem_limit_bytes=used_bytes + SPARE_BYTES

time: 99.4 us -> 96.5 us (0.971)
  Pallas kernels: 98.6 us -> 95.7 us
    pallas_call x1, Pallas kernels: 95.3 us -> 92.5 us  [shards(): pl.pallas_call(functools.partial(kernel, Z, X, E, share), out_shape=shape...]
where the time goes in v4:
time: 96.5 us; the launch traced here: 96.3 us
  Pallas kernels  95.7 us (99%)
    pallas_call x1, Pallas kernels, shards(): pl.pallas_call(functools.partial(kernel, Z, X, E, share), out_shape=shape...  92.5 us
    pallas_call x1, Pallas kernels, shards(): pl.pallas_call(functools.partial(write_out, len(shapes)), out_shape=shape...  3.22 us

profile of v4, /device:TPU:0, one launch (start us, length us, event | category | flops | bytes accessed | tf_op | source)
XLA Modules:
  0.0 96.3 jit_solution(10585408739025162588)
XLA Ops:
  0.6 92.5 %shard_map.75 = (bf16[4,524288]{1,0:T(4,128)(2,1)S(1)}, f32[4,65536]{1,0:T(4,128)S(1)}, f32[4,65536]{1,0:T(4,128)S(1)}, f32[4,65536]{1,0:T(4,128)S(1)}) custom-call(bf16[4,524288]{1,0:T(4,128)(2,1)} %bitcast.8, f32[4,65536]{1,0:T(4,128)} %bitcast.9, f32[4,65536]{1,0:T(4,128)} %bitcast.10, f32[4,65536]{1,0:T(4,128)} %bitcast.11), custom_call_target="tpu_custom_call" | custom-call | tf_op jit(solution)/shard_map/pallas_call | solution.py:720
  93.1 3.2 %shard_map.76 = (bf16[4,524288]{1,0:T(4,128)(2,1)}, f32[4,65536]{1,0:T(4,128)}, f32[4,65536]{1,0:T(4,128)}, f32[4,65536]{1,0:T(4,128)}) custom-call(bf16[4,524288]{1,0:T(4,128)(2,1)S(1)} %get-tuple-element.12.refs_0_, f32[4,65536]{1,0:T(4,128)S(1)} %get-tuple-element.13.refs_1_, f32[4,65536]{1,0:T(4,128)S(1)} %get-tuple-element.14.refs_2_, ...), custom_call_target="tpu_custom_call" | custom-call | tf_op jit(solution)/shard_map/pallas_call | solution.py:754

commit v5 on v4

--- a/solution.py
+++ b/solution.py
@@ -21,7 +21,9 @@
 F32 = jnp.float32
 CHUNKS = 4
 HALF = CHUNKS // 2
-CROSS = CHUNKS // 4
+EARLY = CHUNKS // 4
+LATE = CHUNKS - EARLY
+AHEAD = 4
 PIECES = 8
 SPARE_BYTES = 4 * 1024 * 1024
 BLOCK = 2048
@@ -65,7 +67,7 @@
     Z, X, E, share,
     grads, master_in, first_in, second_in,
     gathered, master, first, second,
-    own, side, xr, pr, xc, raw, chain, code, xcode, exact, mean_grad, squares, norms, coded_state, coded_grad,
+    own, side, xr, pr, xc, raw, chain, code, xcode, exact, mean_grad, squares, norms, coded_state, coded_grad, made_grad,
     own_sem, state_sem, x_send, x_recv, z_send, z_recv,
     p_send, p_recv, q_send, q_recv, r_send, r_recv,
     n_send, n_recv, s_send, s_recv, e_send, e_recv, g_send, g_recv, h_send,
@@ -88,15 +90,34 @@
     raw_pair = jnp.logical_and(inside, jnp.logical_or(pair == 0, pair == Z - 1))
     both_pair = jnp.logical_and(inside, jnp.logical_not(raw_pair))
 
+    far = jnp.where(edge, jnp.where(z == 0, 0, 1), jnp.where(pair < z, 0, 1))
+    rest = CHUNKS - 2
+
+    def in_turn(t):
+        return jnp.where(t < rest, t + 1 + jnp.where(t + 1 >= HALF, 1, 0), (t - rest) * HALF)
+
+    def late_turn(t):
+        return jnp.where(t == 0, HALF, t + jnp.where(t >= HALF, 1, 0))
+
+    def chunk_turn(t):
+        return jnp.where(t == 0, 0, late_turn(t - 1))
+
+    def loop(low, high, act):
+        def body(t, carry):
+            act(t)
+            return carry
+
+        lax.fori_loop(low, high, body, 0)
+
     def own_copy(zz):
         return pltpu.make_async_copy(
             grads.at[:, lanes((zz * X + x) * share, share)], own.at[zz], own_sem.at[zz]
         )
 
     def side_copy(k):
-        start = (z * X + (x + k) % X) * share + HALF * chunk
+        start = (z * X + (x + k) % X) * share + EARLY * chunk
         return pltpu.make_async_copy(
-            grads.at[:, lanes(start, HALF * chunk)], side.at[k - 1], own_sem.at[Z + k - 1]
+            grads.at[:, lanes(start, LATE * chunk)], side.at[k - 1], own_sem.at[Z + k - 1]
         )
 
     states = [
@@ -138,29 +159,43 @@
     def p_copy(k, c):
         return pltpu.make_async_remote_copy(
             src_ref=grads.at[:, lanes((pair * X + (x + k) % X) * share + c * chunk, chunk)],
-            dst_ref=pr.at[k - 1, :, lanes((c - HALF) * chunk, chunk)],
-            send_sem=p_send.at[k - 1, c - HALF],
-            recv_sem=p_recv.at[k - 1, c - HALF],
+            dst_ref=pr.at[k - 1, :, lanes((c - EARLY) * chunk, chunk)],
+            send_sem=p_send.at[k - 1, c - EARLY],
+            recv_sem=p_recv.at[k - 1, c - EARLY],
             device_id=at_dp(pair, x),
             device_id_type=MESH,
         )
 
     def q_copy(k, c):
         return pltpu.make_async_remote_copy(
-            src_ref=xcode.at[k - 1, c - HALF],
-            dst_ref=xc.at[k - 1, c - HALF],
-            send_sem=q_send.at[k - 1, c - HALF],
-            recv_sem=q_recv.at[k - 1, c - HALF],
+            src_ref=xcode.at[k - 1, c - EARLY],
+            dst_ref=xc.at[k - 1, c - EARLY],
+            send_sem=q_send.at[k - 1, c - EARLY],
+            recv_sem=q_recv.at[k - 1, c - EARLY],
             device_id=at_dp(z, (x + k) % X),
             device_id_type=MESH,
         )
 
+    def slot(c):
+        return c - 1 - jnp.where(c > HALF, 1, 0)
+
     def r_copy(c):
         return pltpu.make_async_remote_copy(
             src_ref=grads.at[:, lanes((pair * X + x) * share + c * chunk, chunk)],
-            dst_ref=raw.at[:, lanes((c - HALF) * chunk, chunk)],
-            send_sem=r_send.at[c - HALF],
-            recv_sem=r_recv.at[c - HALF],
+            dst_ref=raw.at[:, lanes(slot(c) * chunk, chunk)],
+            send_sem=r_send.at[slot(c)],
+            recv_sem=r_recv.at[slot(c)],
+            device_id=at_dp(pair, x),
+            device_id_type=MESH,
+        )
+
+    def l_copy(c):
+        toward = jnp.where(pair > z, 1, 0)
+        return pltpu.make_async_remote_copy(
+            src_ref=code.at[z, c],
+            dst_ref=chain.at[toward, z, c],
+            send_sem=z_send.at[z, c],
+            recv_sem=z_recv.at[toward, z, c],
             device_id=at_dp(pair, x),
             device_id_type=MESH,
         )
@@ -202,25 +237,25 @@
 
         def body(c, carry):
             for k in range(1, X):
-                x_copy(zz, k, c).start()
+                x_copy(zz, k, chunk_turn(c)).start()
             return carry
 
-        lax.fori_loop(0, jnp.where(near, HALF, CHUNKS), body, 0)
-
-    def over_late(act):
-        def body(c, carry):
-            act(c)
-            return carry
-
-        lax.fori_loop(HALF, CHUNKS, body, 0)
-
-    @over_late
-    def _(c):
+        lax.fori_loop(0, jnp.where(near, EARLY, CHUNKS), body, 0)
+
+    def send_side(t):
         for k in range(1, X):
-            p_copy(k, c).start()
-
-    for k in range(Z - 1, -1, -1):
+            p_copy(k, late_turn(t)).start()
+
+    loop(0, jnp.where(edge, 2, LATE), send_side)
+    for k in range(Z - 1, 1, -1):
         for_dest(k, start_first)
+    start_first(pair)
+
+    @pl.when(inside)
+    def _():
+        start_first(2 * z - pair)
+
+    start_first(z)
     for k in range(1, X):
         side_copy(k).start()
     for s in states:
@@ -272,7 +307,10 @@
         def send_state(i, carry):
             for j, ref in enumerate((master, first, second)):
                 pack(coded_state.at[j, i], lambda b, ref=ref: part(ref, i * HALF, b))
-                s_copy(j, i).start()
+
+                @pl.when(i * 3 + j < AHEAD)
+                def _(j=j):
+                    s_copy(j, i).start()
             return carry
 
         lax.fori_loop(0, 2, send_state, 0)
@@ -290,12 +328,13 @@
         return block_sum
 
     def hop(zz, c):
-        late = jnp.logical_and(zz == pair, c >= HALF)
+        late = jnp.logical_and(zz == pair, c >= EARLY)
         up = jnp.where(zz > z, 1, 0)
         first = z == (1 - up) * (Z - 1)
         later = jnp.logical_not(first)
-
-        @pl.when(jnp.logical_not(late))
+        sent = jnp.logical_not(jnp.logical_and(first, zz == pair))
+
+        @pl.when(jnp.logical_and(sent, jnp.logical_not(late)))
         def _():
             for k in range(1, X):
                 x_copy(zz, k, c).wait_recv()
@@ -304,7 +343,7 @@
         def _():
             from_chain(up, zz, c).wait_recv()
 
-        @pl.when(jnp.logical_and(first, jnp.logical_not(late)))
+        @pl.when(jnp.logical_and(first, sent))
         def _():
             pack(code.at[zz, c], gather_sum(zz, c, True, ()))
 
@@ -316,9 +355,19 @@
         def _():
             pack(code.at[zz, c], gather_sum(zz, c, False, (up,)))
 
-        @pl.when(jnp.logical_not(jnp.logical_and(first, late)))
+        @pl.when(sent)
         def _():
             z_copy(zz, c).start()
+
+    def send_pairs(t):
+        c = late_turn(t)
+        for j in range(1, X):
+            p_copy(j, c).wait_recv()
+            pack(
+                xcode.at[j - 1, c - EARLY],
+                lambda b: part(side.at[j - 1], c - EARLY, b) + part(pr.at[j - 1], c - EARLY, b),
+            )
+            q_copy(j, c).start()
 
     for k in range(Z - 1, 0, -1):
         for_dest(k, lambda zz: own_copy(zz).wait())
@@ -327,7 +376,10 @@
 
         def body(i, carry, k=k, upper=upper, count=count):
             goes_up = jnp.logical_and(upper, i % count == 0)
-            hop(jnp.where(goes_up, z + k, z - k), i // count)
+            zz = jnp.where(goes_up, z + k, z - k)
+            if k == 1:
+                zz = jnp.where(i % count == 0, pair, 2 * z - pair)
+            hop(zz, chunk_turn(i // count))
             return carry
 
         @pl.when(count > 0)
@@ -335,30 +387,23 @@
             lax.fori_loop(0, CHUNKS * count, body, 0)
 
         if k == Z - 1:
-            @pl.when(edge)
-            def _():
-                over_late(lambda c: r_copy(c).start())
-
             for j in range(1, X):
                 side_copy(j).wait()
-
-            @over_late
-            def _(c):
-                for j in range(1, X):
-                    p_copy(j, c).wait_recv()
-                    pack(
-                        xcode.at[j - 1, c - HALF],
-                        lambda b: part(side.at[j - 1], c - HALF, b) + part(pr.at[j - 1], c - HALF, b),
-                    )
-                    q_copy(j, c).start()
+            loop(0, 2, send_pairs)
+
+        if k == 2:
+            @pl.when(edge)
+            def _():
+                loop(2, LATE, send_side)
+                loop(0, rest, lambda t: r_copy(in_turn(t)).start())
 
     own_copy(z).wait()
     squares[...] = jnp.zeros_like(squares)
 
-    def finish_chunk(c, block_sum):
+    def finish_chunk(c, block_sum, target=mean_grad):
         def body(b, carry):
             mean = block_sum(b) * (1.0 / n)
-            mean_grad[:, lanes(c * chunk + b * BLOCK, BLOCK)] = mean
+            target[:, lanes(c * chunk + b * BLOCK, BLOCK)] = mean
             return carry + mean * mean
 
         squares[...] = lax.fori_loop(0, chunk // BLOCK, body, squares[...])
@@ -369,15 +414,13 @@
         def block_sum(b):
             total = chained(b)
             for k in range(1, X):
-                total = total + unpack(xc.at[k - 1, c - HALF], b)
+                total = total + unpack(xc.at[k - 1, c - EARLY], b)
             if with_raw:
-                total = total + part(raw, c - HALF, b)
+                total = total + part(raw, slot(c), b)
             return total
 
         return block_sum
 
-    far = jnp.where(pair < z, 0, 1)
-    far = jnp.where(edge, jnp.where(z == 0, 0, 1), far)
     def early_finish(c):
         for k in range(1, X):
             x_copy(z, k, c).wait_recv()
@@ -387,11 +430,18 @@
             from_chain(far, z, c).wait_recv()
             finish_chunk(c, gather_sum(z, c, True, (far,)))
 
-        @pl.when(inside)
-        def _():
-            for up in range(2):
-                from_chain(up, z, c).wait_recv()
-            finish_chunk(c, gather_sum(z, c, True, (0, 1)))
+        @pl.when(raw_pair)
+        def _():
+            from_chain(far, z, c).wait_recv()
+            pack(code.at[z, c], gather_sum(z, c, True, (far,)))
+            l_copy(c).start()
+
+        if Z > 4:
+            @pl.when(both_pair)
+            def _():
+                for up in range(2):
+                    from_chain(up, z, c).wait_recv()
+                finish_chunk(c, gather_sum(z, c, True, (0, 1)))
 
     def late_finish(c):
         for k in range(1, X):
@@ -402,7 +452,13 @@
             from_chain(far, z, c).wait_recv()
             finish_chunk(c, late_sum(c, (far,), False))
 
-        @pl.when(raw_pair)
+        @pl.when(jnp.logical_and(raw_pair, c == HALF))
+        def _():
+            from_chain(far, z, c).wait_recv()
+            pack(code.at[z, c], late_sum(c, (far,), False))
+            l_copy(c).start()
+
+        @pl.when(jnp.logical_and(raw_pair, c != HALF))
         def _():
             from_chain(far, z, c).wait_recv()
             r_copy(c).wait_recv()
@@ -415,19 +471,30 @@
                     from_chain(up, z, c).wait_recv()
                 finish_chunk(c, late_sum(c, (0, 1), False))
 
-    def share_grad(i, now=True):
-        @pl.when(jnp.logical_and(raw_pair, now))
-        def _():
-            pack(coded_grad.at[i], lambda b: part(mean_grad, i * HALF, b))
-            e_copy(i).start()
-
-    def finish(c, carry):
-        early_finish(c)
-        share_grad(0, c == 0)
-        late_finish(c + HALF)
+    def finish_for_pair(i, with_x):
+        if with_x:
+            for k in range(1, X):
+                x_copy(pair, k, i * HALF).wait_recv()
+        from_chain(far, pair, i * HALF).wait_recv()
+        finish_chunk(0, gather_sum(pair, i * HALF, with_x, (far,)), made_grad.at[i])
+
+    early_finish(0)
+    loop(2, LATE, send_pairs)
+
+    def finish(t, carry):
+        late_finish(late_turn(t))
+
+        @pl.when(jnp.logical_and(edge, t == 0))
+        def _():
+            finish_for_pair(0, True)
+
+        @pl.when(jnp.logical_and(edge, t == 1))
+        def _():
+            finish_for_pair(1, False)
+
         return carry
 
-    lax.fori_loop(0, HALF, finish, 0)
+    lax.fori_loop(0, LATE, finish, 0)
 
     sums = squares[...]
     while sums.shape[1] > 128:
@@ -453,7 +520,21 @@
             act(n_copy(i, j))
 
     over_others(lambda copy: copy.start())
-    share_grad(1)
+
+    @pl.when(edge)
+    def _():
+        def send_grad(i, carry):
+            pack(coded_grad.at[i], lambda b: part(made_grad.at[i], 0, b))
+            e_copy(i).start()
+            return carry
+
+        lax.fori_loop(0, 2, send_grad, 0)
+
+    @pl.when(raw_pair)
+    def _():
+        for j in range(AHEAD - 3, 3):
+            s_copy(j, 1).start()
+
     over_others(lambda copy: copy.wait_recv())
     total = jnp.full((8, 128), jnp.sum(norms[...]), F32)
     clip_all = jnp.minimum(1.0, clip_limit / (jnp.sqrt(total) + norm_eps))
@@ -488,7 +569,7 @@
         )
 
     def along_x(zz, c, act):
-        @pl.when(jnp.logical_or(zz != pair, c < CROSS))
+        @pl.when(jnp.logical_or(zz != pair, c < EARLY))
         def _():
             for k in range(1, X):
                 act(g_copy(zz, c, k + 1))
@@ -510,6 +591,9 @@
         def _():
             for j in range(3):
                 s_copy(j, i).wait_recv()
+
+        @pl.when(raw_pair)
+        def _():
             e_copy(i).wait_recv()
 
         lax.fori_loop(0, chunk // BLOCK, body, 0)
@@ -518,9 +602,8 @@
     def update_chunk(c, with_params):
         def body(b, inner):
             where = lanes(c * chunk + b * BLOCK, BLOCK)
-            m, f, s = adam_update(
-                mean_grad[:, where], master[:, where], first[:, where], second[:, where], clip_factor
-            )
+            gradient = mean_grad[:, where] if with_params else unpack(coded_grad.at[c // HALF], b)
+            m, f, s = adam_update(gradient, master[:, where], first[:, where], second[:, where], clip_factor)
             master[:, where] = m
             first[:, where] = f
             second[:, where] = s
@@ -530,11 +613,6 @@
 
         lax.fori_loop(0, chunk // BLOCK, body, 0)
 
-    rest = CHUNKS - 2
-
-    def in_turn(t):
-        return jnp.where(t < rest, t + 1 + jnp.where(t + 1 >= HALF, 1, 0), (t - rest) * HALF)
-
     def update(t, carry):
         c = in_turn(t)
         made = jnp.logical_and(raw_pair, t >= rest)
@@ -604,32 +682,36 @@
                     h_copy(k, c).start()
                 return carry
 
-            lax.fori_loop(CROSS, CHUNKS, across, 0)
+            lax.fori_loop(EARLY, CHUNKS, across, 0)
 
     def drain(c, carry):
         for zz in range(Z):
             near = jnp.logical_or(zz == z, zz == pair)
 
-            @pl.when(jnp.logical_not(jnp.logical_and(near, c >= HALF)))
+            @pl.when(jnp.logical_not(jnp.logical_and(near, c >= EARLY)))
             def _():
                 for k in range(1, X):
                     x_copy(zz, k, c).wait_send()
 
-            direct = jnp.logical_and(jnp.logical_and(edge, zz == pair), c >= HALF)
+            direct = jnp.logical_and(edge, zz == pair)
 
             @pl.when(jnp.logical_and(zz != z, jnp.logical_not(direct)))
             def _():
                 z_copy(zz, c).wait_send()
 
-        @pl.when(c >= HALF)
+        @pl.when(c >= EARLY)
         def _():
             for k in range(1, X):
                 p_copy(k, c).wait_send()
                 q_copy(k, c).wait_send()
 
-        @pl.when(jnp.logical_and(c >= HALF, edge))
+        @pl.when(jnp.logical_and(c % HALF != 0, edge))
         def _():
             r_copy(c).wait_send()
+
+        @pl.when(jnp.logical_and(c % HALF == 0, raw_pair))
+        def _():
+            l_copy(c).wait_send()
 
         return carry
 
@@ -640,6 +722,10 @@
         for i in range(2):
             for j in range(3):
                 s_copy(j, i).wait_send()
+
+    @pl.when(edge)
+    def _():
+        for i in range(2):
             e_copy(i).wait_send()
 
     over_others(lambda copy: copy.wait_send())
@@ -651,7 +737,7 @@
                     arrived(zz, (x + k) % X, c)
                 return carry
 
-            lax.fori_loop(0, CROSS if s == 0 else CHUNKS, body, 0)
+            lax.fori_loop(0, EARLY if s == 0 else CHUNKS, body, 0)
 
         for_dest(s, collect)
 
@@ -670,7 +756,7 @@
             def _():
                 g_copy(zz, c, 1).wait_send()
 
-        @pl.when(c >= CROSS)
+        @pl.when(c >= EARLY)
         def _():
             for k in range(1, X):
                 h_copy(k, c).wait_send()
@@ -716,7 +802,7 @@
     arrays = (local_grads[0, 0], master_weights[0], first_moment[0], second_moment[0])
     out_bytes = layers * (2 * flat + 3 * 4 * share)
     coded = share // CHUNKS + 128
-    used_bytes = layers * share * (Z * (2 * X + 3 * 2) + 4 * X + 9) + out_bytes
+    used_bytes = layers * share * (Z * (2 * X + 3 * 2) + 6 * X + 11) + out_bytes
     results = pl.pallas_call(
         functools.partial(kernel, Z, X, E, share),
         out_shape=shapes,
@@ -724,24 +810,25 @@
         out_specs=(local,) * 4,
         scratch_shapes=[
             pltpu.VMEM((Z, layers, share), jnp.bfloat16),
-            pltpu.VMEM((X - 1, layers, share // 2), jnp.bfloat16),
+            pltpu.VMEM((X - 1, layers, LATE * (share // CHUNKS)), jnp.bfloat16),
             pltpu.VMEM((Z, X - 1, layers, share), jnp.bfloat16),
-            pltpu.VMEM((X - 1, layers, share // 2), jnp.bfloat16),
-            pltpu.VMEM((X - 1, HALF, layers, coded), jnp.bfloat16),
+            pltpu.VMEM((X - 1, layers, LATE * (share // CHUNKS)), jnp.bfloat16),
+            pltpu.VMEM((X - 1, LATE, layers, coded), jnp.bfloat16),
             pltpu.VMEM((layers, share // 2), jnp.bfloat16),
             pltpu.VMEM((2, Z, CHUNKS, layers, coded), jnp.bfloat16),
             pltpu.VMEM((Z, CHUNKS, layers, coded), jnp.bfloat16),
-            pltpu.VMEM((X - 1, HALF, layers, coded), jnp.bfloat16),
+            pltpu.VMEM((X - 1, LATE, layers, coded), jnp.bfloat16),
             pltpu.VMEM((layers, share // CHUNKS), F32),
             pltpu.VMEM((layers, share), F32),
             pltpu.VMEM((layers, BLOCK), F32),
             pltpu.VMEM((n * E, 1, 128), F32),
             pltpu.VMEM((3, 2, layers, coded), jnp.bfloat16),
             pltpu.VMEM((2, layers, coded), jnp.bfloat16),
+            pltpu.VMEM((2, layers, share // CHUNKS), F32),
             dma((Z + X - 1,)), dma((3,)),
             dma((Z, X - 1, CHUNKS)), dma((Z, X - 1, CHUNKS)),
             dma((Z, CHUNKS)), dma((2, Z, CHUNKS)),
-            dma((X - 1, HALF)), dma((X - 1, HALF)), dma((X - 1, HALF)), dma((X - 1, HALF)),
+            dma((X - 1, LATE)), dma((X - 1, LATE)), dma((X - 1, LATE)), dma((X - 1, LATE)),
             dma((HALF,)), dma((HALF,)),
             dma((n * E,)), dma((n * E,)),
             dma((3, 2)), dma((3, 2)), dma((2,)), dma((2,)),

time: 96.5 us -> 94.1 us (0.975)
  Pallas kernels: 95.7 us -> 93.3 us
    pallas_call x1, Pallas kernels: 92.5 us -> 90.1 us  [shards(): pl.pallas_call(functools.partial(kernel, Z, X, E, share), out_shape=shape...]
where the time goes in v5:
time: 94.1 us; the launch traced here: 94 us
  Pallas kernels  93.3 us (99%)
    pallas_call x1, Pallas kernels, shards(): pl.pallas_call(functools.partial(kernel, Z, X, E, share), out_shape=shape...  90.1 us
    pallas_call x1, Pallas kernels, shards(): pl.pallas_call(functools.partial(write_out, len(shapes)), out_shape=shape...  3.22 us

profile of v5, /device:TPU:0, one launch (start us, length us, event | category | flops | bytes accessed | tf_op | source)
XLA Modules:
  0.0 94.0 jit_solution(17487317080416677312)
XLA Ops:
  0.6 90.1 %shard_map.75 = (bf16[4,524288]{1,0:T(4,128)(2,1)S(1)}, f32[4,65536]{1,0:T(4,128)S(1)}, f32[4,65536]{1,0:T(4,128)S(1)}, f32[4,65536]{1,0:T(4,128)S(1)}) custom-call(bf16[4,524288]{1,0:T(4,128)(2,1)} %bitcast.8, f32[4,65536]{1,0:T(4,128)} %bitcast.9, f32[4,65536]{1,0:T(4,128)} %bitcast.10, f32[4,65536]{1,0:T(4,128)} %bitcast.11), custom_call_target="tpu_custom_call" | custom-call | tf_op jit(solution)/shard_map/pallas_call | solution.py:806
  90.7 3.2 %shard_map.76 = (bf16[4,524288]{1,0:T(4,128)(2,1)}, f32[4,65536]{1,0:T(4,128)}, f32[4,65536]{1,0:T(4,128)}, f32[4,65536]{1,0:T(4,128)}) custom-call(bf16[4,524288]{1,0:T(4,128)(2,1)S(1)} %get-tuple-element.12.refs_0_, f32[4,65536]{1,0:T(4,128)S(1)} %get-tuple-element.13.refs_1_, f32[4,65536]{1,0:T(4,128)S(1)} %get-tuple-element.14.refs_2_, ...), custom_call_target="tpu_custom_call" | custom-call | tf_op jit(solution)/shard_map/pallas_call | solution.py:841

commit v6 on v5

--- a/solution.py
+++ b/solution.py
@@ -26,7 +26,7 @@
 AHEAD = 4
 PIECES = 8
 SPARE_BYTES = 4 * 1024 * 1024
-BLOCK = 2048
+BLOCK = 4096
 SPAN = 250.0
 TINY = 1e-35
 

time: 94.1 us -> 93.9 us (level)
  no operation moved by 1% of the time
where the time goes in v6:
time: 93.9 us; the launch traced here: 93.7 us
  Pallas kernels  93.1 us (99%)
    pallas_call x1, Pallas kernels, shards(): pl.pallas_call(functools.partial(kernel, Z, X, E, share), out_shape=shape...  89.9 us
    pallas_call x1, Pallas kernels, shards(): pl.pallas_call(functools.partial(write_out, len(shapes)), out_shape=shape...  3.22 us

profile of v6, /device:TPU:0, one launch (start us, length us, event | category | flops | bytes accessed | tf_op | source)
XLA Modules:
  0.0 93.7 jit_solution(6707249289006507136)
XLA Ops:
  0.6 89.9 %shard_map.75 = (bf16[4,524288]{1,0:T(4,128)(2,1)S(1)}, f32[4,65536]{1,0:T(4,128)S(1)}, f32[4,65536]{1,0:T(4,128)S(1)}, f32[4,65536]{1,0:T(4,128)S(1)}) custom-call(bf16[4,524288]{1,0:T(4,128)(2,1)} %bitcast.8, f32[4,65536]{1,0:T(4,128)} %bitcast.9, f32[4,65536]{1,0:T(4,128)} %bitcast.10, f32[4,65536]{1,0:T(4,128)} %bitcast.11), custom_call_target="tpu_custom_call" | custom-call | tf_op jit(solution)/shard_map/pallas_call | solution.py:806
  90.5 3.2 %shard_map.76 = (bf16[4,524288]{1,0:T(4,128)(2,1)}, f32[4,65536]{1,0:T(4,128)}, f32[4,65536]{1,0:T(4,128)}, f32[4,65536]{1,0:T(4,128)}) custom-call(bf16[4,524288]{1,0:T(4,128)(2,1)S(1)} %get-tuple-element.12.refs_0_, f32[4,65536]{1,0:T(4,128)S(1)} %get-tuple-element.13.refs_1_, f32[4,65536]{1,0:T(4,128)S(1)} %get-tuple-element.14.refs_2_, ...), custom_call_target="tpu_custom_call" | custom-call | tf_op jit(solution)/shard_map/pallas_call | solution.py:841
